TPU v7x, 256 devices: a whole 4x4x8 slice. The times are simulated.
256 devices in a mesh: gx: 4 (over y_lo, core), gz: 8 (over y_hi, x), ta: 8 (over z).
Axes of the slice: x: 4, y: 4 (y_hi: 2, y_lo: 2; y = y_hi * 2 + y_lo), z: 8, core: 2. Of those that a mesh axis runs over, the one named last changes fastest.
Arguments:
- links: float32 [4, 2, 3, 3, 32, 32, 512], P(None, None, None, None, 'ta', 'gz', 'gx'), may hold values from -1 to 1, as said below
Outputs:
- force: float32 [4, 2, 3, 3, 32, 32, 512], P(None, None, None, None, 'ta', 'gz', 'gx')
Inputs may be any that keep to these rules, and one draw needn't show every extreme that they name: Every link matrix (real part links[mu, 0], imaginary part links[mu, 1]) is special unitary, up to float32 rounding.
All inputs are finite; a program needn't handle non-finite values.
Results may differ from a plain program's by a relative error of at most 0.0003.
Values sent between devices are 32-bit elements; how exact they have to be, the bound alone decides.
A program may use at most 64 MiB of HBM per device.

v0:
```python
import functools

import jax
import jax.numpy as jnp
from jax import lax
from jax.experimental import pallas as pl
from jax.experimental.pallas import tpu as pltpu
from jax.sharding import PartitionSpec as P

NX = 16
COEFF = -1.9
AXES = ("ta", "gz", "gx")
SUB, LANES = 8, 128


def others(d):
    return [m for m in range(4) if m != d]


class Lattice:
    def __init__(self, depth):
        self.depth = depth
        self.per = SUB // depth
        self.ygroups = LANES // NX
        self.row = lax.broadcasted_iota(jnp.int32, (SUB, LANES), 0)
        self.lane = lax.broadcasted_iota(jnp.int32, (SUB, LANES), 1)
        self.zrow = self.row % depth
        self.xcol = self.lane % NX

    def rows(self, value, shift):
        shift %= SUB
        return pltpu.roll(value, shift, 0) if shift else value

    def lanes(self, value, shift):
        shift %= LANES
        return pltpu.roll(value, shift, 1) if shift else value


def entry(left, right, i, j, part, left_h, right_h):
    total = None
    for k in range(3):
        li = (k, i) if left_h else (i, k)
        ri = (j, k) if right_h else (k, j)
        lr, lm = left[0][li[0]][li[1]], left[1][li[0]][li[1]]
        rr, rm = right[0][ri[0]][ri[1]], right[1][ri[0]][ri[1]]
        if part == 0:
            first, second = lr * rr, lm * rm
            minus = left_h == right_h
        elif left_h:
            first, second = lr * rm, lm * rr
            minus = True
        else:
            first, second = lm * rr, lr * rm
            minus = right_h
        value = first - second if minus else first + second
        total = value if total is None else total + value
    return total


def product(left, right, left_h=False, right_h=False):
    return [
        [[entry(left, right, i, j, part, left_h, right_h) for j in range(3)] for i in range(3)]
        for part in range(2)
    ]


def projected(left, right, left_h=False, right_h=False):
    get = lambda i, j, part: entry(left, right, i, j, part, left_h, right_h)
    pairs = ((0, 1), (0, 2), (1, 2))
    real = [get(i, j, 0) - get(j, i, 0) for i, j in pairs]
    imag = [get(i, j, 1) + get(j, i, 1) for i, j in pairs]
    diag = [get(i, i, 1) for i in range(3)]
    third = (diag[0] + diag[1] + diag[2]) * (1.0 / 3.0)
    return real + imag + [diag[0] - third, diag[1] - third]


def third_row(real, imag):
    rows_r, rows_i = [], []
    for column in range(3):
        n, l = (column + 1) % 3, (column + 2) % 3
        rows_r.append(
            real[0][n] * real[1][l]
            - imag[0][n] * imag[1][l]
            - real[0][l] * real[1][n]
            + imag[0][l] * imag[1][n]
        )
        rows_i.append(
            real[0][l] * imag[1][n]
            + imag[0][l] * real[1][n]
            - real[0][n] * imag[1][l]
            - imag[0][n] * real[1][l]
        )
    return rows_r, rows_i


def sizes(depth, halves):
    yg = LANES // NX
    per = SUB // depth

    def rows(count):
        return (
            -(-count // per) * SUB,
            -(-count // depth) * SUB * halves,
            -(-count // yg) * SUB * halves,
        )

    return rows(36), rows(24)


PLANES = ((2, 3), (1, 3), (1, 2), (0, 1), (0, 2), (0, 3))


def force_terms(
    counts, depth, halves, hbm, acc,
    u, ahead_s, local_s, plaq_s, st, sz, sy, rt, rz, ry, qz, qy, pz, py, bs, br, ezs, ezr, eys, eyr,
    load_sem, send, recv,
):
    g = Lattice(depth)
    me = [lax.axis_index(a) for a in AXES]
    nxt = [lax.rem(me[i] + 1, counts[i]) for i in range(3)]
    prv = [lax.rem(me[i] + counts[i] - 1, counts[i]) for i in range(3)]

    def device(i, index):
        where = list(me)
        where[i] = index
        by = dict(zip(AXES, where))
        return (by["gx"], by["gz"], by["ta"])

    def diagonal(time, i, index):
        where = list(me)
        where[0], where[i] = time, index
        by = dict(zip(AXES, where))
        return (by["gx"], by["gz"], by["ta"])

    barrier = pltpu.get_barrier_semaphore()
    for i in (1, 2):
        for where in (diagonal(nxt[0], i, prv[i]), diagonal(prv[0], i, nxt[i])):
            pl.semaphore_signal(
                barrier, inc=1, device_id=where, device_id_type=pl.DeviceIdType.MESH
            )
    for i in range(3):
        for index in (nxt[i], prv[i]):
            pl.semaphore_signal(
                barrier, inc=1, device_id=device(i, index), device_id_type=pl.DeviceIdType.MESH
            )

    loads = {
        m: pltpu.make_async_copy(hbm.at[m, :, 0:2], u.at[m, :, 0:2], load_sem.at[m])
        for m in range(4)
    }
    last_rows = pltpu.make_async_copy(hbm.at[:, :, 2], u.at[:, :, 2], load_sem.at[4])
    for m in (3, 2, 1, 0):
        loads[m].start()
    last_rows.start()

    def load(m, part, i, j, h):
        return u[m, part, i, j, h * SUB : (h + 1) * SUB, :]

    def comps(d, m):
        return [(m, part, i, j) for part in range(2) for i in range(2) for j in range(3)]

    def all_comps(d):
        return [c for m in others(d) for c in comps(d, m)]

    def pack_t(m):
        cs, base = comps(0, m), 12 * others(0).index(m)
        for c0 in range(0, 12, g.per):
            value = None
            for k in range(g.per):
                x = g.rows(load(*cs[c0 + k], 0), depth * k)
                value = x if value is None else jnp.where(g.row >= depth * k, x, value)
            r = (base + c0) // g.per * SUB
            st[r : r + SUB, :] = value

    def pack_z(m):
        cs, base = comps(1, m), 12 * others(1).index(m)
        for c0 in range(0, 12, depth):
            for h in range(halves):
                value = None
                for k in range(depth):
                    x = g.rows(load(*cs[c0 + k], h), k)
                    value = x if value is None else jnp.where(g.zrow >= k, x, value)
                r = ((base + c0) // depth * halves + h) * SUB
                sz[r : r + SUB, :] = value

    def pack_y():
        cs = all_comps(2)
        for c0 in range(0, len(cs), g.ygroups):
            for h in range(halves):
                value = None
                for k in range(min(g.ygroups, len(cs) - c0)):
                    x = g.lanes(load(*cs[c0 + k], h), NX * k)
                    value = x if value is None else jnp.where(g.lane >= NX * k, x, value)
                r = (c0 // g.ygroups * halves + h) * SUB
                sy[r : r + SUB, :] = value

    def pack_back(m):
        cs = comps(0, m)
        for c0 in range(0, 12, g.per):
            value = None
            for k in range(g.per):
                x = g.rows(load(*cs[c0 + k], halves - 1), depth * (k + 1))
                value = x if value is None else jnp.where(g.row >= depth * k, x, value)
            r = (12 * m + c0) // g.per * SUB
            bs[r : r + SUB, :] = value

    def pack_edges():
        cs = comps(0, 0)
        for c0 in range(0, 12, SUB):
            rows = lanes = None
            for k in range(min(SUB, 12 - c0)):
                v = load(*cs[c0 + k], halves - 1)
                x = g.rows(v, k - (SUB - depth))
                rows = x if rows is None else jnp.where(g.row >= k, x, rows)
            ezs[c0 : c0 + SUB, :] = rows
        for c0 in range(0, 12, g.ygroups):
            for k in range(min(g.ygroups, 12 - c0)):
                x = g.lanes(g.rows(load(*cs[c0 + k], halves - 1), depth), NX * k)
                lanes = x if k == 0 else jnp.where(g.lane >= NX * k, x, lanes)
            r = c0 // g.ygroups * SUB
            eys[r : r + SUB, :] = lanes

    for m in (3, 2, 1, 0):
        loads[m].wait()
        pack_back(m)
        if m != 0:
            pack_t(m)
        if m != 1:
            pack_z(m)
    pack_y()
    pack_edges()

    def remote(src, dst, slot, i, index):
        return pltpu.make_async_remote_copy(
            src_ref=src, dst_ref=dst, send_sem=send.at[slot], recv_sem=recv.at[slot],
            device_id=device(i, index), device_id_type=pl.DeviceIdType.MESH,
        )

    def chunk(ref, d, m):
        n = ref.shape[0] // 3
        k = others(d).index(m)
        return ref.at[k * n : (k + 1) * n]

    first, second = {}, {}
    slot = 0
    for d, m in ((0, 1), (0, 2), (0, 3), (1, 3), (1, 2), (1, 0), (2, None)):
        src, dst = ((st, rt), (sz, rz), (sy, ry))[d]
        if m is not None:
            src, dst = chunk(src, d, m), chunk(dst, d, m)
        first[d, m] = remote(src, dst, slot, d, prv[d])
        slot += 1
    back = {}
    for m in range(4):
        n = bs.shape[0] // 4
        back[m] = remote(bs.at[m * n : (m + 1) * n], br.at[m * n : (m + 1) * n], slot, 0, nxt[0])
        slot += 1
    for i, src, dst in ((1, ezs, ezr), (2, eys, eyr)):
        back["edge", i] = pltpu.make_async_remote_copy(
            src_ref=src, dst_ref=dst, send_sem=send.at[slot], recv_sem=recv.at[slot],
            device_id=diagonal(nxt[0], i, prv[i]), device_id_type=pl.DeviceIdType.MESH,
        )
        slot += 1
    for d in (1, 2):
        src, dst = (None, (qz, pz), (qy, py))[d]
        for m in others(d):
            second[d, m] = remote(chunk(src, d, m), chunk(dst, d, m), slot, d, nxt[d])
            slot += 1

    pl.semaphore_wait(barrier, 10)
    for key, copy in first.items():
        if key[0]:
            copy.start()
    low_faces = [copy for key, copy in first.items() if not key[0]]
    high_faces = [back[key] for key in (("edge", 1), ("edge", 2), 0, 3, 2, 1)]
    around = me[0] == counts[0] - 1

    @pl.when(around)
    def _():
        for copy in high_faces + low_faces:
            copy.start()

    @pl.when(jnp.logical_not(around))
    def _():
        for copy in low_faces + high_faces:
            copy.start()

    last_rows.wait()

    def matrix(m, h):
        return [[[load(m, part, i, j, h) for j in range(3)] for i in range(3)] for part in range(2)]

    def save(ref, index, value):
        for part in range(2):
            for i in range(len(value[part])):
                for j in range(3):
                    ref[index, part, i, j] = value[part][i][j]

    def saved(ref, index, rows=3):
        return [[[ref[index, part, i, j] for j in range(3)] for i in range(rows)] for part in range(2)]

    def rolled(m, d, h, part, i, j):
        v = load(m, part, i, j, h)
        if d == 3:
            return jnp.where(g.xcol == NX - 1, g.lanes(v, NX - 1), g.lanes(v, -1))
        if d == 2:
            return g.lanes(v, -NX)
        if d == 1:
            return g.rows(v, -1)
        if h + 1 < halves:
            beyond = g.rows(load(m, part, i, j, h + 1), -depth)
            return jnp.where(g.row >= SUB - depth, beyond, g.rows(v, -depth))
        return g.rows(v, -depth)

    def complete(d, h):
        return d == 3 or (d == 0 and h + 1 < halves)

    slots = {}
    for mu, nu in PLANES:
        for h in range(halves):
            for m, d in ((nu, mu), (mu, nu)):
                slots[m, d, h] = len(slots)
                rows = 3 if complete(d, h) else 2
                save(
                    ahead_s, slots[m, d, h],
                    [[[rolled(m, d, h, part, i, j) for j in range(3)] for i in range(rows)] for part in range(2)],
                )
            save(
                local_s, PLANES.index((mu, nu)) * halves + h,
                product(matrix(mu, h), matrix(nu, h), left_h=True),
            )

    def ahead(m, d, h):
        if complete(d, h):
            return saved(ahead_s, slots[m, d, h])
        index = {c: n for n, c in enumerate(all_comps(d))}

        def get(part, i, j):
            v = ahead_s[slots[m, d, h], part, i, j]
            c = index[(m, part, i, j)]
            if d == 0:
                r = c // g.per * SUB
                edge = g.rows(rt[r : r + SUB, :], SUB - depth - depth * (c % g.per))
                return jnp.where(g.row >= SUB - depth, edge, v)
            if d == 1:
                r = (c // depth * halves + h) * SUB
                edge = g.rows(rz[r : r + SUB, :], depth - 1 - c % depth)
                return jnp.where(g.zrow == depth - 1, edge, v)
            r = (c // g.ygroups * halves + h) * SUB
            edge = g.lanes(ry[r : r + SUB, :], LANES - NX - NX * (c % g.ygroups))
            return jnp.where(g.lane >= LANES - NX, edge, v)

        real = [[get(0, i, j) for j in range(3)] for i in range(2)]
        imag = [[get(1, i, j) for j in range(3)] for i in range(2)]
        third_r, third_i = third_row(real, imag)
        return [real + [third_r], imag + [third_i]]

    seen = set()

    def add(m, c, h, value):
        r = ((m * 8 + c) * halves + h) * SUB
        if (m, c, h) in seen:
            acc[r : r + SUB, :] += value
        else:
            seen.add((m, c, h))
            acc[r : r + SUB, :] = value

    def lower(m, d, h, q):
        base = others(d).index(m) * 8
        if d == 2:
            for c0 in range(0, 8, g.ygroups):
                value = None
                for k in range(g.ygroups):
                    x = g.lanes(q[c0 + k], NX * (k + 1))
                    value = x if value is None else jnp.where(g.lane >= NX * k, x, value)
                r = ((base + c0) // g.ygroups * halves + h) * SUB
                qy[r : r + SUB, :] = value
        elif d == 1:
            for c0 in range(0, 8, depth):
                value = None
                for k in range(depth):
                    x = g.rows(q[c0 + k], k + 1 - depth)
                    value = x if value is None else jnp.where(g.zrow >= k, x, value)
                r = ((base + c0) // depth * halves + h) * SUB
                qz[r : r + SUB, :] = value
        for c in range(8):
            if d == 3:
                add(m, c, h, jnp.where(g.xcol == 0, g.lanes(q[c], 1 - NX), g.lanes(q[c], 1)))
            elif d == 2:
                add(m, c, h, jnp.where(g.lane >= NX, g.lanes(q[c], NX), 0.0))
            elif d == 1:
                add(m, c, h, jnp.where(g.zrow > 0, g.rows(q[c], 1), 0.0))
            else:
                moved = g.rows(q[c], depth)
                add(m, c, h, jnp.where(g.row >= depth, moved, 0.0))
                if h + 1 < halves:
                    add(m, c, h + 1, jnp.where(g.row < depth, moved, 0.0))

    steps = [(pair, h) for pair in PLANES if pair[0] for h in range(halves)]
    steps += [(pair, h) for h in range(halves) for pair in PLANES if not pair[0]]
    arrived, left = set(), {key: halves for key in second}
    for (mu, nu), h in steps:
        n = PLANES.index((mu, nu))
        for d, m in ((mu, nu), (nu, mu)):
            key = (d, None if d == 2 else m)
            if key in first and key not in arrived and not complete(d, h):
                arrived.add(key)
                first[key].wait_recv()
        a = product(ahead(nu, mu, h), ahead(mu, nu, h), right_h=True)
        save(plaq_s, n * halves + h, a)
        b = saved(local_s, n * halves + h)
        lower(mu, nu, h, projected(a, b, left_h=True))
        lower(nu, mu, h, projected(a, b, right_h=True))
        for key in ((mu, nu), (nu, mu)):
            if key in second:
                left[key] -= 1
                if not left[key]:
                    second[key].start()

    for n, (mu, nu) in enumerate(PLANES):
        for h in range(halves):
            e = product(matrix(mu, h), saved(plaq_s, n * halves + h))
            upper = projected(e, matrix(nu, h), right_h=True)
            for c in range(8):
                add(mu, c, h, upper[c])
                add(nu, c, h, -upper[c])

    def complete_rows(get):
        real = [[get(0, i, j) for j in range(3)] for i in range(2)]
        imag = [[get(1, i, j) for j in range(3)] for i in range(2)]
        third_r, third_i = third_row(real, imag)
        return [real + [third_r], imag + [third_i]]

    def behind(m):
        def get(part, i, j):
            c = 12 * m + part * 6 + i * 3 + j
            r = c // g.per * SUB
            return g.rows(br[r : r + SUB, :], -depth * (c % g.per))

        return complete_rows(get)

    for key in (("edge", 1), ("edge", 2), 0):
        back[key].wait_recv()
    time_link = behind(0)
    for m in (3, 2, 1):
        back[m].wait_recv()

        def step(part, i, j):
            v = time_link[part][i][j]
            c = part * 6 + i * 3 + j
            if m == 3:
                return jnp.where(g.xcol == NX - 1, g.lanes(v, NX - 1), g.lanes(v, -1))
            if m == 1:
                r = c // SUB * SUB
                edge = g.rows(ezr[r : r + SUB, :], depth - 1 - c % SUB)
                return jnp.where(g.row == depth - 1, edge, g.rows(v, -1))
            r = c // g.ygroups * SUB
            edge = g.lanes(eyr[r : r + SUB, :], LANES - NX - NX * (c % g.ygroups))
            return jnp.where(g.lane >= LANES - NX, edge, g.lanes(v, -NX))

        a = product(matrix(m, 0), complete_rows(step), right_h=True)
        b = product(time_link, behind(m), left_h=True)
        q = projected(a, b, right_h=True)
        for c in range(8):
            add(m, c, 0, jnp.where(g.row < depth, q[c], 0.0))

    for m in (3, 2, 1, 0):
        for d in others(m):
            if d in (1, 2):
                second[d, m].wait_recv()
        for h in range(halves):
            for c in range(8):
                r = ((m * 8 + c) * halves + h) * SUB
                value = acc[r : r + SUB, :]
                for d in others(m):
                    b = others(d).index(m) * 8 + c
                    if d == 1:
                        s = (b // depth * halves + h) * SUB
                        x = g.rows(pz[s : s + SUB, :], -(b % depth))
                        value = value + jnp.where(g.zrow == 0, x, 0.0)
                    elif d == 2:
                        s = (b // g.ygroups * halves + h) * SUB
                        x = g.lanes(py[s : s + SUB, :], -NX * (b % g.ygroups))
                        value = value + jnp.where(g.lane < NX, x, 0.0)
                acc[r : r + SUB, :] = value
    for copy in list(first.values()) + list(back.values()) + list(second.values()):
        copy.wait_send()


def expand(halves, acc, hbm, out, sems):
    copies = []
    for m in range(4):
        for h in range(halves):
            rows = [((m * 8 + c) * halves + h) * SUB for c in range(8)]
            f = [acc[r : r + SUB, :] * (COEFF * 0.5 if c < 6 else COEFF) for c, r in enumerate(rows)]

            def put(part, i, j, value):
                out[m, part, i, j, h * SUB : (h + 1) * SUB, :] = value

            for n, (i, j) in enumerate(((0, 1), (0, 2), (1, 2))):
                put(0, i, j, f[n])
                put(0, j, i, -f[n])
                put(1, i, j, f[3 + n])
                put(1, j, i, f[3 + n])
            for i in range(3):
                put(0, i, i, jnp.zeros((SUB, LANES), jnp.float32))
            put(1, 0, 0, f[6])
            put(1, 1, 1, f[7])
            put(1, 2, 2, -(f[6] + f[7]))
        copies.append(pltpu.make_async_copy(out.at[m], hbm.at[m], sems.at[m]))
        copies[-1].start()
    for copy in copies:
        copy.wait()


def per_device(counts, links):
    time_len, depth, flat = links.shape[4:]
    sites = time_len * depth
    assert flat == LANES and SUB % depth == 0 and sites % SUB == 0
    halves = sites // SUB
    rows1, rows2 = sizes(depth, halves)
    vmem = lambda *s: pltpu.VMEM(s + (LANES,), jnp.float32)
    shape = links.shape[:4] + (sites, flat)
    terms = pl.pallas_call(
        functools.partial(force_terms, counts, depth, halves),
        out_shape=pltpu.VMEM((32 * sites, flat), jnp.float32),
        in_specs=[pl.BlockSpec(memory_space=pl.ANY)],
        out_specs=pl.BlockSpec(memory_space=pltpu.VMEM),
        scratch_shapes=[
            vmem(*shape[:-1]),
            vmem(12 * halves, 2, 3, 3, SUB),
            vmem(6 * halves, 2, 3, 3, SUB),
            vmem(6 * halves, 2, 3, 3, SUB),
        ]
        + [vmem(r) for r in rows1 + rows1 + rows2[1:] + rows2[1:]]
        + [vmem(r) for r in (rows1[0] // 3 * 4,) * 2 + (2 * SUB,) * 4]
        + [
            pltpu.SemaphoreType.DMA((5,)),
            pltpu.SemaphoreType.DMA((19,)),
            pltpu.SemaphoreType.DMA((19,)),
        ],
        compiler_params=pltpu.CompilerParams(collective_id=0, has_side_effects=True),
        name="force_terms",
    )(links.reshape(shape))
    out = pl.pallas_call(
        functools.partial(expand, halves),
        out_shape=jax.ShapeDtypeStruct(shape, jnp.float32),
        in_specs=[pl.BlockSpec(memory_space=pltpu.VMEM)],
        out_specs=pl.BlockSpec(memory_space=pl.ANY),
        scratch_shapes=[vmem(*shape[:-1]), pltpu.SemaphoreType.DMA((4,))],
        name="expand",
    )(pltpu.with_memory_space_constraint(terms, pltpu.VMEM))
    return out.reshape(links.shape)


def solution(mesh):
    assert mesh.axis_names == ("gx", "gz", "ta")
    counts = tuple(mesh.shape[a] for a in AXES)
    spec = P(None, None, None, None, "ta", "gz", "gx")
    return jax.shard_map(
        functools.partial(per_device, counts),
        mesh=mesh,
        in_specs=(spec,),
        out_specs=spec,
        check_vma=False,
    )
```

profile of v0, /device:TPU:1, one launch (start us, length us, event | category | flops | bytes accessed | tf_op | source)
XLA Modules:
  0.0 20.6 jit_solution(1556720432912778365)
XLA Ops:
  0.0 19.7 %force_terms.1.acc = f32[512,128]{1,0:T(8,128)S(1)} custom-call(f32[4,2,3,3,16,128]{5,4,3,2,1,0:T(8,128)} %bitcast.2), custom_call_target="tpu_custom_call" | custom-call | tf_op jit(solution)/shard_map/force_terms/pallas_call | solution.py:523
  19.7 0.9 %expand.1 = f32[4,2,3,3,16,128]{5,4,3,2,1,0:T(8,128)} custom-call(f32[512,128]{1,0:T(8,128)S(1)} %force_terms.1.acc), custom_call_target="tpu_custom_call" | custom-call | tf_op jit(solution)/shard_map/expand/pallas_call | solution.py:544
where the time goes:
time: 20.7 us; the launch traced here: 20.6 us
  Pallas kernels  20.6 us (100%)
    pallas_call x1, Pallas kernels, per_device(): pl.pallas_call(functools.partial(force_terms, counts, depth, halves), out...  19.7 us
    pallas_call x1, Pallas kernels, per_device(): pl.pallas_call(functools.partial(expand, halves), out_shape=jax.ShapeDtyp...  0.86 us

commit v1 on v0

v1 whole, which is shorter than its diff:
```python
import functools

import jax
import jax.numpy as jnp
from jax import lax
from jax.experimental import pallas as pl
from jax.experimental.pallas import tpu as pltpu
from jax.sharding import PartitionSpec as P

NX = 16
COEFF = -1.9
AXES = ("ta", "gz", "gx")
SUB, LANES = 8, 128


def others(d):
    return [m for m in range(4) if m != d]


class Lattice:
    def __init__(self, depth):
        self.depth = depth
        self.per = SUB // depth
        self.ygroups = LANES // NX
        self.row = lax.broadcasted_iota(jnp.int32, (SUB, LANES), 0)
        self.lane = lax.broadcasted_iota(jnp.int32, (SUB, LANES), 1)
        self.zrow = self.row % depth
        self.xcol = self.lane % NX

    def rows(self, value, shift):
        shift %= SUB
        return pltpu.roll(value, shift, 0) if shift else value

    def lanes(self, value, shift):
        shift %= LANES
        return pltpu.roll(value, shift, 1) if shift else value


def entry(left, right, i, j, part, left_h, right_h):
    total = None
    for k in range(3):
        li = (k, i) if left_h else (i, k)
        ri = (j, k) if right_h else (k, j)
        lr, lm = left[0][li[0]][li[1]], left[1][li[0]][li[1]]
        rr, rm = right[0][ri[0]][ri[1]], right[1][ri[0]][ri[1]]
        if part == 0:
            first, second = lr * rr, lm * rm
            minus = left_h == right_h
        elif left_h:
            first, second = lr * rm, lm * rr
            minus = True
        else:
            first, second = lm * rr, lr * rm
            minus = right_h
        value = first - second if minus else first + second
        total = value if total is None else total + value
    return total


def product(left, right, left_h=False, right_h=False):
    return [
        [[entry(left, right, i, j, part, left_h, right_h) for j in range(3)] for i in range(3)]
        for part in range(2)
    ]


def projected(left, right, left_h=False, right_h=False):
    get = lambda i, j, part: entry(left, right, i, j, part, left_h, right_h)
    pairs = ((0, 1), (0, 2), (1, 2))
    real = [get(i, j, 0) - get(j, i, 0) for i, j in pairs]
    imag = [get(i, j, 1) + get(j, i, 1) for i, j in pairs]
    diag = [get(i, i, 1) for i in range(3)]
    third = (diag[0] + diag[1] + diag[2]) * (1.0 / 3.0)
    return real + imag + [diag[0] - third, diag[1] - third]


def third_row(real, imag):
    rows_r, rows_i = [], []
    for column in range(3):
        n, l = (column + 1) % 3, (column + 2) % 3
        rows_r.append(
            real[0][n] * real[1][l]
            - imag[0][n] * imag[1][l]
            - real[0][l] * real[1][n]
            + imag[0][l] * imag[1][n]
        )
        rows_i.append(
            real[0][l] * imag[1][n]
            + imag[0][l] * real[1][n]
            - real[0][n] * imag[1][l]
            - imag[0][n] * real[1][l]
        )
    return rows_r, rows_i


PLANES = ((2, 3), (0, 3), (0, 2), (1, 3), (1, 2), (0, 1))
DIAGONALS = ((0, 1), (1, 0), (0, 2), (2, 0), (1, 2), (2, 1))


def force_terms(
    counts, depth, halves, hbm, acc,
    u, ahead_s, local_s, pre_s, xs0, xs1, xs2, xr0, xr1, xr2, gs0, gs1, gs2, gr0, gr1, gr2, es, er,
    load_sem, send, recv,
):
    g = Lattice(depth)
    me = [lax.axis_index(a) for a in AXES]
    xs, xr, gs, gr = (xs0, xs1, xs2), (xr0, xr1, xr2), (gs0, gs1, gs2), (gr0, gr1, gr2)

    def device(*steps):
        where = list(me)
        for i, step in steps:
            where[i] = lax.rem(me[i] + (step + counts[i]), counts[i])
        by = dict(zip(AXES, where))
        return (by["gx"], by["gz"], by["ta"])

    barrier = pltpu.get_barrier_semaphore()
    partners = [device((i, step)) for i in (1, 0, 2) for step in (1, -1)]
    partners += [device((d, 1), (n, -1)) for d, n in DIAGONALS]
    for where in partners:
        pl.semaphore_signal(barrier, inc=1, device_id=where, device_id_type=pl.DeviceIdType.MESH)

    loads = [
        pltpu.make_async_copy(hbm.at[m], u.at[m], load_sem.at[m]) for m in range(4)
    ]
    for m in (1, 0, 2, 3):
        loads[m].start()

    def load(m, part, i, j, h):
        return u[m, part, i, j, h * SUB : (h + 1) * SUB, :]

    comps = [(part, i, j) for part in range(2) for i in range(2) for j in range(3)]

    def slot(d, m, n, h):
        k = others(d).index(m)
        if d == 0:
            return k * 48 + n // g.per * SUB, n % g.per
        if d == 1:
            return k * 48 + (n // depth * halves + h) * SUB, n % depth
        return k * 32 + (n // g.ygroups * halves + h) * SUB, n % g.ygroups

    def group(d):
        return (g.per, depth, g.ygroups)[d]

    def shifted(d, value, steps):
        if d == 0:
            return g.rows(value, depth * steps)
        return g.rows(value, steps) if d == 1 else g.lanes(value, NX * steps)

    def place(d):
        return (g.row // depth, g.zrow, g.lane // NX)[d]

    def pack(ref, d, m, h, get, layer):
        for n0 in range(0, 12, group(d)):
            value = None
            for n in range(n0, min(12, n0 + group(d))):
                r, k = slot(d, m, n, h)
                x = shifted(d, get(*comps[n]), k - layer)
                value = x if value is None else jnp.where(place(d) >= k, x, value)
            ref[r : r + SUB, :] = value

    def unpack(ref, d, m, n, h, layer):
        r, k = slot(d, m, n, h)
        return shifted(d, ref[r : r + SUB, :], layer - k)

    last = [g.per - 1, depth - 1, g.ygroups - 1]

    def face_halves(d, top):
        return range(halves) if d else ((halves - 1,) if top else (0,))

    def pack_faces(d):
        for m in others(d):
            for h in face_halves(d, False):
                pack(xs[d], d, m, h, lambda part, i, j: load(m, part, i, j, h), 0)

    def pack_edges(d, n):
        r0 = DIAGONALS.index((d, n)) * 2 * SUB
        layout = 1 if 2 not in (d, n) else 2
        for c0 in range(0, 12, SUB):
            value = None
            for k in range(min(SUB, 12 - c0)):
                c = comps[c0 + k]
                if layout == 1:
                    v = load(d, *c, halves - 1 if d == 0 else 0)
                    x = g.rows(v, k - depth if d == 0 else k - (depth - 1))
                    value = x if value is None else jnp.where(g.row >= k, x, value)
                    continue
                if 0 in (d, n):
                    v = load(d, *c, halves - 1 if d == 0 else 0)
                else:
                    at = depth - 1 if d == 1 else 0
                    step = -1 if d == 1 else 1
                    v = load(d, *c, 0)
                    for h in range(1, halves):
                        v = jnp.where(g.zrow == at + step * h, g.rows(load(d, *c, h), step * h), v)
                x = g.lanes(v, NX * (k + (1 if d == 2 else 0)))
                value = x if value is None else jnp.where(g.lane >= NX * k, x, value)
            es[r0 + c0 : r0 + c0 + SUB, :] = value

    def edge(d, n, h):
        r0 = DIAGONALS.index((d, n)) * 2 * SUB

        def get(part, i, j):
            c = part * 6 + i * 3 + j
            v = er[r0 + c // SUB * SUB : r0 + c // SUB * SUB + SUB, :]
            k = c % SUB
            if (d, n) == (0, 1):
                return g.rows(v, depth - 1 - k)
            if (d, n) == (1, 0):
                return g.rows(v, SUB - depth - k)
            v = g.lanes(v, NX * ((0 if d == 2 else g.ygroups - 1) - k))
            if (d, n) == (0, 2):
                return g.rows(v, -(SUB - depth))
            if (d, n) == (2, 0):
                return g.rows(v, SUB - depth)
            return g.rows(v, 1 - depth + h if d == 1 else depth - 1 - h)

        return complete_rows(get)

    def complete_rows(get):
        real = [[get(0, i, j) for j in range(3)] for i in range(2)]
        imag = [[get(1, i, j) for j in range(3)] for i in range(2)]
        third_r, third_i = third_row(real, imag)
        return [real + [third_r], imag + [third_i]]

    def matrix(m, h):
        return [[[load(m, part, i, j, h) for j in range(3)] for i in range(3)] for part in range(2)]

    def save(ref, index, value):
        for part in range(2):
            for i in range(len(value[part])):
                for j in range(3):
                    ref[index, part, i, j] = value[part][i][j]

    def saved(ref, index):
        return [[[ref[index, part, i, j] for j in range(3)] for i in range(3)] for part in range(2)]

    def rolled(m, d, h, part, i, j):
        v = load(m, part, i, j, h)
        if d == 3:
            return jnp.where(g.xcol == NX - 1, g.lanes(v, NX - 1), g.lanes(v, -1))
        if d == 2:
            return g.lanes(v, -NX)
        if d == 1:
            return g.rows(v, -1)
        if h + 1 < halves:
            beyond = g.rows(load(m, part, i, j, h + 1), -depth)
            return jnp.where(g.row >= SUB - depth, beyond, g.rows(v, -depth))
        return g.rows(v, -depth)

    def complete(d, h):
        return d == 3 or (d == 0 and h + 1 < halves)

    def top(d, h):
        if d == 0:
            return g.row >= SUB - depth
        return g.zrow == depth - 1 if d == 1 else g.lane >= LANES - NX

    def index(m, d, h):
        return (m * 4 + d) * halves + h

    def save_local(mu, nu):
        for h in range(halves):
            for m, d in ((nu, mu), (mu, nu)):
                save(
                    ahead_s, index(m, d, h),
                    [[[rolled(m, d, h, part, i, j) for j in range(3)] for i in range(3)] for part in range(2)],
                )
            save(
                local_s, PLANES.index((mu, nu)) * halves + h,
                product(matrix(mu, h), matrix(nu, h), left_h=True),
            )

    def pack_open(d):
        for m in others(d):
            mu, nu = min(d, m), max(d, m)
            for h in face_halves(d, True):
                b = saved(local_s, PLANES.index((mu, nu)) * halves + h)
                v = saved(ahead_s, index(d, m, h))

                def get(part, i, j):
                    value = entry(b, v, i, j, part, d > m, False)
                    if complete(m, h):
                        return value
                    if d < m:
                        short = b[part][i][j]
                    else:
                        short = b[0][j][i] if part == 0 else -b[1][j][i]
                    return jnp.where(top(m, h), short, value)

                pack(gs[d], d, m, h, get, last[d])

    def remote(src, dst, where):
        n = len(copies)
        copies.append(
            pltpu.make_async_remote_copy(
                src_ref=src, dst_ref=dst, send_sem=send.at[n], recv_sem=recv.at[n],
                device_id=where, device_id_type=pl.DeviceIdType.MESH,
            )
        )
        return copies[-1]

    def chunk(ref, d, m):
        n = ref.shape[0] // 3
        k = others(d).index(m)
        return ref.at[k * n : (k + 1) * n]

    copies, faces, opens, edges = [], {}, {}, {}
    for d, n in DIAGONALS:
        r = DIAGONALS.index((d, n)) * 2 * SUB
        rows = slice(r, r + 2 * SUB)
        edges[d, n] = remote(es.at[rows], er.at[rows], device((d, 1), (n, -1)))
    for d in range(3):
        for m in others(d):
            faces[d, m] = remote(chunk(xs[d], d, m), chunk(xr[d], d, m), device((d, -1)))
            opens[d, m] = remote(chunk(gs[d], d, m), chunk(gr[d], d, m), device((d, 1)))

    for m in (1, 0, 2, 3):
        loads[m].wait()
    pack_faces(1)
    for pair in PLANES:
        if 1 in pair:
            save_local(*pair)
    pack_open(1)
    for d, n in DIAGONALS:
        pack_edges(d, n)
    pl.semaphore_wait(barrier, len(partners))
    for key in ((1, 2), (2, 1), (0, 1), (1, 0), (0, 2), (2, 0)):
        edges[key].start()
    for m in (3, 2, 0):
        faces[1, m].start()
        opens[1, m].start()
    pack_faces(0)
    for m in (3, 2, 1):
        faces[0, m].start()
    pack_faces(2)
    for m in (3, 0, 1):
        faces[2, m].start()
    for pair in PLANES:
        if 1 not in pair:
            save_local(*pair)
    pack_open(0)
    for m in (3, 2, 1):
        opens[0, m].start()
    pack_open(2)
    for m in (3, 0, 1):
        opens[2, m].start()

    def ahead(m, d, h):
        if complete(d, h):
            return saved(ahead_s, index(m, d, h))

        def get(part, i, j):
            v = ahead_s[index(m, d, h), part, i, j]
            return jnp.where(top(d, h), unpack(xr[d], d, m, comps.index((part, i, j)), h, last[d]), v)

        return complete_rows(get)

    seen = set()

    def add(m, c, h, value):
        r = ((m * 8 + c) * halves + h) * SUB
        if (m, c, h) in seen:
            acc[r : r + SUB, :] += value
        else:
            seen.add((m, c, h))
            acc[r : r + SUB, :] = value

    def lower(m, d, h, q):
        for c in range(8):
            if d == 3:
                add(m, c, h, jnp.where(g.xcol == 0, g.lanes(q[c], 1 - NX), g.lanes(q[c], 1)))
            elif d == 2:
                add(m, c, h, jnp.where(g.lane >= NX, g.lanes(q[c], NX), 0.0))
            elif d == 1:
                add(m, c, h, jnp.where(g.zrow > 0, g.rows(q[c], 1), 0.0))
            else:
                moved = g.rows(q[c], depth)
                add(m, c, h, jnp.where(g.row >= depth, moved, 0.0))
                if h + 1 < halves:
                    add(m, c, h + 1, jnp.where(g.row < depth, moved, 0.0))

    arrived = set()

    def plane(mu, nu):
        for h in range(halves):
            n = PLANES.index((mu, nu)) * halves + h
            for d, m in ((mu, nu), (nu, mu)):
                if (d, m) not in arrived and not complete(d, h):
                    arrived.add((d, m))
                    faces[d, m].wait_recv()
            a = product(ahead(nu, mu, h), ahead(mu, nu, h), right_h=True)
            b = saved(local_s, n)
            lower(mu, nu, h, projected(a, b, left_h=True))
            lower(nu, mu, h, projected(a, b, right_h=True))
            e = product(matrix(mu, h), a)
            upper = projected(e, matrix(nu, h), right_h=True)
            for c in range(8):
                add(mu, c, h, upper[c])
                add(nu, c, h, -upper[c])

    def edge_mask(d, m, h):
        if m == 2:
            return g.lane >= LANES - NX
        if m == 1:
            return g.zrow == depth - 1
        return g.row >= SUB - depth

    def has_edge(d, m, h):
        return m in (1, 2) or (m == 0 and h == halves - 1)

    def prepare(d, m):
        if m != 3:
            edges[d, m].wait_recv()
        for h in face_halves(d, False):
            if has_edge(d, m, h):
                own = matrix(m, h)
                both = product(own, edge(d, m, h), right_h=True)
                save(
                    pre_s, index(m, d, h),
                    [
                        [
                            [jnp.where(edge_mask(d, m, h), both[p][i][j], own[p][i][j]) for j in range(3)]
                            for i in range(3)
                        ]
                        for p in range(2)
                    ],
                )

    def close(d, m):
        opens[d, m].wait_recv()
        for h in face_halves(d, False):
            own = saved(pre_s, index(m, d, h)) if has_edge(d, m, h) else matrix(m, h)
            back = complete_rows(
                lambda part, i, j: unpack(gr[d], d, m, comps.index((part, i, j)), h, 0)
            )
            q = projected(own, back, right_h=True)
            mask = (g.row < depth, g.zrow == 0, g.lane < NX)[d]
            for c in range(8):
                add(m, c, h, jnp.where(mask, q[c], 0.0))

    for pair in PLANES[:3]:
        plane(*pair)
    for d, m in ((0, 3), (2, 3), (0, 2), (2, 0), (0, 1), (2, 1)):
        prepare(d, m)
        close(d, m)
    for m in (3, 2, 0):
        prepare(1, m)
    for pair in PLANES[3:]:
        plane(*pair)
    for m in (3, 2, 0):
        close(1, m)
    for copy in copies:
        copy.wait_send()


def expand(halves, acc, hbm, out, sems):
    copies = []
    for m in range(4):
        for h in range(halves):
            rows = [((m * 8 + c) * halves + h) * SUB for c in range(8)]
            f = [acc[r : r + SUB, :] * (COEFF * 0.5 if c < 6 else COEFF) for c, r in enumerate(rows)]

            def put(part, i, j, value):
                out[m, part, i, j, h * SUB : (h + 1) * SUB, :] = value

            for n, (i, j) in enumerate(((0, 1), (0, 2), (1, 2))):
                put(0, i, j, f[n])
                put(0, j, i, -f[n])
                put(1, i, j, f[3 + n])
                put(1, j, i, f[3 + n])
            for i in range(3):
                put(0, i, i, jnp.zeros((SUB, LANES), jnp.float32))
            put(1, 0, 0, f[6])
            put(1, 1, 1, f[7])
            put(1, 2, 2, -(f[6] + f[7]))
        copies.append(pltpu.make_async_copy(out.at[m], hbm.at[m], sems.at[m]))
        copies[-1].start()
    for copy in copies:
        copy.wait()


def per_device(counts, links):
    time_len, depth, flat = links.shape[4:]
    sites = time_len * depth
    assert flat == LANES and (time_len, depth) == (4, 4)
    halves = sites // SUB
    faces = (144, 144, 96)
    vmem = lambda *s: pltpu.VMEM(s + (LANES,), jnp.float32)
    shape = links.shape[:4] + (sites, flat)
    terms = pl.pallas_call(
        functools.partial(force_terms, counts, depth, halves),
        out_shape=pltpu.VMEM((32 * sites, flat), jnp.float32),
        in_specs=[pl.BlockSpec(memory_space=pl.ANY)],
        out_specs=pl.BlockSpec(memory_space=pltpu.VMEM),
        scratch_shapes=[
            vmem(*shape[:-1]),
            vmem(16 * halves, 2, 3, 3, SUB),
            vmem(6 * halves, 2, 3, 3, SUB),
            vmem(16 * halves, 2, 3, 3, SUB),
        ]
        + [vmem(r) for r in faces * 4]
        + [vmem(6 * 2 * SUB)] * 2
        + [
            pltpu.SemaphoreType.DMA((4,)),
            pltpu.SemaphoreType.DMA((24,)),
            pltpu.SemaphoreType.DMA((24,)),
        ],
        compiler_params=pltpu.CompilerParams(collective_id=0, has_side_effects=True),
        name="force_terms",
    )(links.reshape(shape))
    out = pl.pallas_call(
        functools.partial(expand, halves),
        out_shape=jax.ShapeDtypeStruct(shape, jnp.float32),
        in_specs=[pl.BlockSpec(memory_space=pltpu.VMEM)],
        out_specs=pl.BlockSpec(memory_space=pl.ANY),
        scratch_shapes=[vmem(*shape[:-1]), pltpu.SemaphoreType.DMA((4,))],
        name="expand",
    )(pltpu.with_memory_space_constraint(terms, pltpu.VMEM))
    return out.reshape(links.shape)


def solution(mesh):
    assert mesh.axis_names == ("gx", "gz", "ta")
    counts = tuple(mesh.shape[a] for a in AXES)
    spec = P(None, None, None, None, "ta", "gz", "gx")
    return jax.shard_map(
        functools.partial(per_device, counts),
        mesh=mesh,
        in_specs=(spec,),
        out_specs=spec,
        check_vma=False,
    )
```

time: 20.7 us -> 18.1 us (0.87)
  Pallas kernels: 20.6 us -> 18 us
    pallas_call x1, Pallas kernels: 19.7 us -> 17.2 us  [per_device(): pl.pallas_call(functools.partial(force_terms, counts, depth, halves), out...]
where the time goes in v1:
time: 18.1 us; the launch traced here: 18 us
  Pallas kernels  18 us (99%)
    pallas_call x1, Pallas kernels, per_device(): pl.pallas_call(functools.partial(force_terms, counts, depth, halves), out...  17.2 us
    pallas_call x1, Pallas kernels, per_device(): pl.pallas_call(functools.partial(expand, halves), out_shape=jax.ShapeDtyp...  0.86 us

profile of v1, /device:TPU:1, one launch (start us, length us, event | category | flops | bytes accessed | tf_op | source)
XLA Modules:
  0.0 18.0 jit_solution(9742810988864655109)
XLA Ops:
  0.0 17.2 %force_terms.1.acc = f32[512,128]{1,0:T(8,128)S(1)} custom-call(f32[4,2,3,3,16,128]{5,4,3,2,1,0:T(8,128)} %bitcast.2), custom_call_target="tpu_custom_call" | custom-call | tf_op jit(solution)/shard_map/force_terms/pallas_call | solution.py:490
  17.2 0.9 %expand.1 = f32[4,2,3,3,16,128]{5,4,3,2,1,0:T(8,128)} custom-call(f32[512,128]{1,0:T(8,128)S(1)} %force_terms.1.acc), custom_call_target="tpu_custom_call" | custom-call | tf_op jit(solution)/shard_map/expand/pallas_call | solution.py:511

commit v2 on v1

v2 whole, which is shorter than its diff:
```python
import functools

import jax
import jax.numpy as jnp
from jax import lax
from jax.experimental import pallas as pl
from jax.experimental.pallas import tpu as pltpu
from jax.sharding import PartitionSpec as P

NX = 16
COEFF = -1.9
AXES = ("ta", "gz", "gx")
SUB, LANES = 8, 128


def others(d):
    return [m for m in range(4) if m != d]


class Lattice:
    def __init__(self, depth):
        self.depth = depth
        self.per = SUB // depth
        self.ygroups = LANES // NX
        self.row = lax.broadcasted_iota(jnp.int32, (SUB, LANES), 0)
        self.lane = lax.broadcasted_iota(jnp.int32, (SUB, LANES), 1)
        self.zrow = self.row % depth
        self.xcol = self.lane % NX

    def rows(self, value, shift):
        shift %= SUB
        return pltpu.roll(value, shift, 0) if shift else value

    def lanes(self, value, shift):
        shift %= LANES
        return pltpu.roll(value, shift, 1) if shift else value


def entry(left, right, i, j, part, left_h, right_h):
    total = None
    for k in range(3):
        li = (k, i) if left_h else (i, k)
        ri = (j, k) if right_h else (k, j)
        lr, lm = left[0][li[0]][li[1]], left[1][li[0]][li[1]]
        rr, rm = right[0][ri[0]][ri[1]], right[1][ri[0]][ri[1]]
        if part == 0:
            first, second = lr * rr, lm * rm
            minus = left_h == right_h
        elif left_h:
            first, second = lr * rm, lm * rr
            minus = True
        else:
            first, second = lm * rr, lr * rm
            minus = right_h
        value = first - second if minus else first + second
        total = value if total is None else total + value
    return total


def product(left, right, left_h=False, right_h=False):
    return [
        [[entry(left, right, i, j, part, left_h, right_h) for j in range(3)] for i in range(3)]
        for part in range(2)
    ]


def projected(left, right, left_h=False, right_h=False):
    get = lambda i, j, part: entry(left, right, i, j, part, left_h, right_h)
    pairs = ((0, 1), (0, 2), (1, 2))
    real = [get(i, j, 0) - get(j, i, 0) for i, j in pairs]
    imag = [get(i, j, 1) + get(j, i, 1) for i, j in pairs]
    diag = [get(i, i, 1) for i in range(3)]
    third = (diag[0] + diag[1] + diag[2]) * (1.0 / 3.0)
    return real + imag + [diag[0] - third, diag[1] - third]


def third_row(real, imag):
    rows_r, rows_i = [], []
    for column in range(3):
        n, l = (column + 1) % 3, (column + 2) % 3
        rows_r.append(
            real[0][n] * real[1][l]
            - imag[0][n] * imag[1][l]
            - real[0][l] * real[1][n]
            + imag[0][l] * imag[1][n]
        )
        rows_i.append(
            real[0][l] * imag[1][n]
            + imag[0][l] * real[1][n]
            - real[0][n] * imag[1][l]
            - imag[0][n] * real[1][l]
        )
    return rows_r, rows_i


PLANES = ((0, 1), (0, 2), (0, 3), (1, 2), (1, 3), (2, 3))
DIAGONALS = ((0, 2), (2, 0), (0, 1), (1, 0), (1, 2), (2, 1))
LAYOUT = (
    (((1, 0), (2, 0)), ((3, 0),)),
    (((0, 0), (0, 1), (2, 0), (2, 1)), ((3, 0), (3, 1))),
    (((0, 0), (0, 1), (1, 0), (1, 1), (3, 0), (3, 1)),),
)
ROWS = (144, 144, 96)
EDGE = 2 * SUB


def offset(kind, d):
    if kind == "e":
        return 2 * sum(ROWS) + d * EDGE
    return (sum(ROWS) if kind == "g" else 0) + sum(ROWS[:d])


TOTAL = offset("e", len(DIAGONALS))


def force_terms(
    counts, depth, halves, hbm, acc, u, out_s, in_s, face_s, b_s, pre_s, load_sem, send, recv,
):
    g = Lattice(depth)
    me = [lax.axis_index(a) for a in AXES]
    comps = [(part, i, j) for part in range(2) for i in range(2) for j in range(3)]
    last = (g.per - 1, depth - 1, g.ygroups - 1)
    place = (g.row // depth, g.zrow, g.lane // NX)

    def device(*steps):
        where = list(me)
        for i, step in steps:
            where[i] = lax.rem(me[i] + (step + counts[i]), counts[i])
        by = dict(zip(AXES, where))
        return (by["gx"], by["gz"], by["ta"])

    loads = [
        pltpu.make_async_copy(hbm.at[m, part], u.at[m, part], load_sem)
        for m in range(4)
        for part in range(2)
    ]
    for copy in loads:
        copy.start()
    barrier = pltpu.get_barrier_semaphore()
    partners = [device((i, step)) for i in (1, 0, 2) for step in (1, -1)]
    partners += [device((d, 1), (n, -1)) for d, n in DIAGONALS]
    for where in partners:
        pl.semaphore_signal(barrier, inc=1, device_id=where, device_id_type=pl.DeviceIdType.MESH)

    def remote(start, rows, slot, where):
        span = slice(start, start + rows)
        return pltpu.make_async_remote_copy(
            src_ref=out_s.at[span], dst_ref=in_s.at[span], send_sem=send, recv_sem=recv.at[slot],
            device_id=where, device_id_type=pl.DeviceIdType.MESH,
        )

    faces = [remote(offset("x", d), ROWS[d], d, device((d, -1))) for d in range(3)]
    opens = [remote(offset("g", d), ROWS[d], 3 + d, device((d, 1))) for d in range(3)]
    edges = [
        remote(offset("e", k), EDGE, 6 if k < 2 else 7, device((d, 1), (n, -1)))
        for k, (d, n) in enumerate(DIAGONALS)
    ]
    near_edges = remote(offset("e", 0), 2 * EDGE, 6, partners[0])
    far_edges = remote(offset("e", 2), 4 * EDGE, 7, partners[0])
    everything = remote(0, TOTAL, 0, partners[0])

    def load(m, part, i, j, h):
        return u[m, part, i, j, h * SUB : (h + 1) * SUB, :]

    def shifted(d, value, steps):
        if d == 0:
            return g.rows(value, depth * steps)
        return g.rows(value, steps) if d == 1 else g.lanes(value, NX * steps)

    def half(d, h, top):
        return (halves - 1 if top else 0) if d == 0 else h

    def complete(d, h):
        return d == 3 or (d == 0 and h + 1 < halves)

    def top(d, h=1):
        if d == 0:
            return g.row >= SUB - depth
        return g.zrow == depth - 1 if d == 1 else g.lane >= LANES - NX

    def bottom(d):
        return (g.row < depth, g.zrow == 0, g.lane < NX)[d]

    def open_mask(d, s, among=(0, 1, 2)):
        mask = None
        for k, (m, h) in enumerate(LAYOUT[d][s]):
            if m in among and not complete(m, h if d else 1):
                here = jnp.logical_and(place[d] == k, top(m))
                mask = here if mask is None else jnp.logical_or(mask, here)
        return mask

    def pick(mask, yes, no):
        return no if mask is None else jnp.where(mask, yes, no)

    def pack(d, s, get, up):
        value = None
        for k, (m, h) in enumerate(LAYOUT[d][s]):
            x = get(m, half(d, h, up))
            if x is None:
                continue
            x = shifted(d, x, k - (last[d] if up else 0))
            value = x if value is None else jnp.where(place[d] >= k, x, value)
        return value

    def complete_rows(get):
        real = [[get(0, i, j) for j in range(3)] for i in range(2)]
        imag = [[get(1, i, j) for j in range(3)] for i in range(2)]
        third_r, third_i = third_row(real, imag)
        return [real + [third_r], imag + [third_i]]

    def packed(d, s, get, up):
        return complete_rows(
            lambda part, i, j: pack(d, s, lambda m, h: get(m, h, part, i, j), up)
        )

    def put(kind, d, s, value):
        r = offset(kind, d)
        used = len(LAYOUT[d][s])
        for n, (part, i, j) in enumerate(comps[: 6 if s else 12]):
            v = value[part][i][j]
            if s:
                v = jnp.where(place[d] < used, v, shifted(d, value[1][i][j], used))
            at = r + (96 if s else 0) + n * SUB
            out_s[at : at + SUB, :] = v

    def fetch(ref, kind, d, s, part, i, j):
        n = part * 6 + i * 3 + j
        at = offset(kind, d) + n * SUB
        if not s:
            return ref[at : at + SUB, :]
        at += 96 - part * 6 * SUB
        v = ref[at : at + SUB, :]
        return shifted(d, v, -len(LAYOUT[d][s])) if part else v

    def fetched(ref, kind, d, s):
        return complete_rows(lambda part, i, j: fetch(ref, kind, d, s, part, i, j))

    def rolled(m, d, h, part, i, j):
        v = load(m, part, i, j, h)
        if d == 3:
            return jnp.where(g.xcol == NX - 1, g.lanes(v, NX - 1), g.lanes(v, -1))
        if d == 2:
            return g.lanes(v, -NX)
        if d == 1:
            return g.rows(v, -1)
        if h + 1 < halves:
            beyond = g.rows(load(m, part, i, j, h + 1), -depth)
            return jnp.where(g.row >= SUB - depth, beyond, g.rows(v, -depth))
        return g.rows(v, -depth)

    def matrix(get):
        return [[[get(part, i, j) for j in range(3)] for i in range(3)] for part in range(2)]

    def save(ref, index, value):
        for part in range(2):
            for i in range(ref.shape[-4]):
                for j in range(3):
                    ref[(*index, part, i, j)] = value[part][i][j]

    sets = [(d, s) for d in range(3) for s in range(len(LAYOUT[d]))]

    def kept(d, s, q):
        n = sets.index((d, s))
        return complete_rows(lambda part, i, j: face_s[n, q, part, i, j])

    def send_side(d):
        own = packed(d, 0, lambda m, h, *c: load(d, *c, h), True)
        for s in range(len(LAYOUT[d])):
            n = sets.index((d, s))
            side = packed(d, s, lambda m, h, *c: load(m, *c, h), True)
            over = packed(d, s, lambda m, h, *c: rolled(d, m, h, *c), True)
            b = product(own, side, left_h=True)
            mask = open_mask(d, s)
            put("g", d, s, [
                [
                    [pick(mask, b[p][i][j], entry(b, over, i, j, p, False, False)) for j in range(3)]
                    for i in range(2)
                ]
                for p in range(2)
            ])
            for q, value in enumerate((own, side, over)):
                save(face_s, (n, q), value)
            save(b_s, (n,), b)
            put("x", d, s, [
                [
                    [pack(d, s, lambda m, h: load(m, p, i, j, h), False) for j in range(3)]
                    for i in range(2)
                ]
                for p in range(2)
            ])

    def pack_edges(d, n):
        r0 = offset("e", DIAGONALS.index((d, n)))
        for c0 in range(0, 12, SUB):
            value = None
            for k in range(min(SUB, 12 - c0)):
                c = comps[c0 + k]
                if 2 not in (d, n):
                    v = load(d, *c, halves - 1 if d == 0 else 0)
                    x = g.rows(v, k - depth if d == 0 else k - (depth - 1))
                    value = x if value is None else jnp.where(g.row >= k, x, value)
                    continue
                if 0 in (d, n):
                    v = load(d, *c, halves - 1 if d == 0 else 0)
                else:
                    at = depth - 1 if d == 1 else 0
                    step = -1 if d == 1 else 1
                    v = load(d, *c, 0)
                    for h in range(1, halves):
                        v = jnp.where(g.zrow == at + step * h, g.rows(load(d, *c, h), step * h), v)
                x = g.lanes(v, NX * (k + (1 if d == 2 else 0)))
                value = x if value is None else jnp.where(g.lane >= NX * k, x, value)
            out_s[r0 + c0 : r0 + c0 + SUB, :] = value

    def edge(d, n, h, part, i, j):
        c = part * 6 + i * 3 + j
        r = offset("e", DIAGONALS.index((d, n))) + c // SUB * SUB
        v = in_s[r : r + SUB, :]
        k = c % SUB
        if (d, n) == (0, 1):
            return g.rows(v, depth - 1 - k)
        if (d, n) == (1, 0):
            return g.rows(v, SUB - depth - k)
        v = g.lanes(v, NX * ((0 if d == 2 else g.ygroups - 1) - k))
        if (d, n) == (0, 2):
            return g.rows(v, -(SUB - depth))
        if (d, n) == (2, 0):
            return g.rows(v, SUB - depth)
        return g.rows(v, 1 - depth + h if d == 1 else depth - 1 - h)

    everything_in = pltpu.make_async_copy(hbm, u, load_sem)
    everything_in.wait()
    for d in (1, 0, 2):
        send_side(d)
    for d, n in DIAGONALS:
        pack_edges(d, n)
    pl.semaphore_wait(barrier, len(partners))
    for copy in [opens[1], faces[1]] + edges[2:] + [opens[0], faces[0], opens[2], faces[2]] + edges[:2]:
        copy.start()

    seen, pending = set(), {}

    def add(m, c, h, value):
        key = (m, c, h)
        pending[key] = pending[key] + value if key in pending else value

    def flush():
        for (m, c, h), value in pending.items():
            r = ((m * 8 + c) * halves + h) * SUB
            if (m, c, h) in seen:
                acc[r : r + SUB, :] += value
            else:
                seen.add((m, c, h))
                acc[r : r + SUB, :] = value
        pending.clear()

    def forward(m, d, h, q):
        for c in range(8):
            if d == 3:
                add(m, c, h, jnp.where(g.xcol == 0, g.lanes(q[c], 1 - NX), g.lanes(q[c], 1)))
            elif d == 2:
                add(m, c, h, g.lanes(q[c], NX))
            elif d == 1:
                add(m, c, h, g.rows(q[c], 1))
            elif h + 1 < halves:
                moved = g.rows(q[c], depth)
                add(m, c, h, jnp.where(g.row >= depth, moved, 0.0))
                add(m, c, h + 1, jnp.where(g.row < depth, moved, 0.0))
            else:
                add(m, c, h, g.rows(q[c], depth))

    def masked(mask, a):
        return [[[pick(mask, 0.0, v) for v in line] for line in part] for part in a]

    def inner(mu, nu, h):
        own = matrix(lambda *c: load(mu, *c, h))
        side = matrix(lambda *c: load(nu, *c, h))
        a = product(
            matrix(lambda *c: rolled(nu, mu, h, *c)),
            matrix(lambda *c: rolled(mu, nu, h, *c)),
            right_h=True,
        )
        mask = None
        for d in (mu, nu):
            if not complete(d, h):
                mask = top(d) if mask is None else jnp.logical_or(mask, top(d))
        a = masked(mask, a)
        b = product(own, side, left_h=True)
        forward(mu, nu, h, projected(a, b, left_h=True))
        forward(nu, mu, h, projected(a, b, right_h=True))
        upper = projected(product(own, a), side, right_h=True)
        for c in range(8):
            add(mu, c, h, upper[c])
            add(nu, c, h, -upper[c])

    def corners(d, among):
        for s in range(len(LAYOUT[d])):
            mask = open_mask(d, s, among)
            if mask is None:
                continue
            n = sets.index((d, s))

            def corner(m, h, c):
                if m not in among or complete(m, h):
                    return None
                k = LAYOUT[m][0].index((d, 0 if m == 0 else h))
                return shifted(m, fetch(in_s, "x", m, 0, *c), last[m] - k)

            for c in comps:
                value = pack(d, s, lambda m, h: corner(m, h, c), True)
                face_s[(n, 2, *c)] = jnp.where(mask, value, face_s[(n, 2, *c)])

    def face_terms(d, closed):
        for s, spots in enumerate(LAYOUT[d]):
            n = sets.index((d, s))
            own, side, over = (kept(d, s, q) for q in range(3))
            a = product(fetched(in_s, "x", d, s), over, right_h=True)
            a = masked(open_mask(d, s, [m for m in range(3) if m not in closed]), a)
            b = matrix(lambda *c: b_s[(n, *c)])
            upper = projected(product(own, a), side, right_h=True)
            low = projected(a, b, left_h=True)
            mask = open_mask(d, s, closed)
            low = [pick(mask, 0.0, v) for v in low]
            for k, (m, h) in enumerate(spots):
                h = half(d, h, True)
                natural = lambda v: jnp.where(top(d), shifted(d, v, last[d] - k), 0.0)
                for c in range(8):
                    x = natural(upper[c])
                    add(d, c, h, x)
                    add(m, c, h, -x)
                forward(d, m, h, [natural(v) for v in low])
        flush()

    def prepare(d):
        for s in range(len(LAYOUT[d])):
            own = fetched(out_s, "x", d, s)
            mask = open_mask(d, s)
            if mask is not None:
                far = packed(
                    d, s,
                    lambda m, h, *c: None if complete(m, h if d else 1) else edge(d, m, h, *c),
                    False,
                )
                both = product(own, far, right_h=True)
                own = [
                    [[jnp.where(mask, both[p][i][j], own[p][i][j]) for j in range(3)] for i in range(3)]
                    for p in range(2)
                ]
            save(pre_s, (sets.index((d, s)),), own)

    def close(d):
        for s, spots in enumerate(LAYOUT[d]):
            n = sets.index((d, s))
            q = projected(
                matrix(lambda *c: pre_s[(n, *c)]), fetched(in_s, "g", d, s), right_h=True
            )
            for k, (m, h) in enumerate(spots):
                for c in range(8):
                    add(m, c, half(d, h, False), jnp.where(bottom(d), shifted(d, q[c], -k), 0.0))
        flush()

    for pair in PLANES:
        for h in range(halves):
            inner(*pair, h)
        flush()
    faces[2].wait_recv()
    face_terms(2, ())
    corners(0, (2,))
    faces[0].wait_recv()
    face_terms(0, (2,))
    corners(1, (0, 2))
    near_edges.wait_recv()
    far_edges.wait_recv()
    for d in (2, 0, 1):
        prepare(d)
    for d in (2, 0):
        opens[d].wait_recv()
        close(d)
    faces[1].wait_recv()
    face_terms(1, (0, 2))
    opens[1].wait_recv()
    close(1)
    everything.wait_send()


def expand(halves, acc, hbm, out, sems):
    copies = []
    for m in range(4):
        for h in range(halves):
            rows = [((m * 8 + c) * halves + h) * SUB for c in range(8)]
            f = [acc[r : r + SUB, :] * (COEFF * 0.5 if c < 6 else COEFF) for c, r in enumerate(rows)]

            def put(part, i, j, value):
                out[m, part, i, j, h * SUB : (h + 1) * SUB, :] = value

            for n, (i, j) in enumerate(((0, 1), (0, 2), (1, 2))):
                put(0, i, j, f[n])
                put(0, j, i, -f[n])
                put(1, i, j, f[3 + n])
                put(1, j, i, f[3 + n])
            for i in range(3):
                put(0, i, i, jnp.zeros((SUB, LANES), jnp.float32))
            put(1, 0, 0, f[6])
            put(1, 1, 1, f[7])
            put(1, 2, 2, -(f[6] + f[7]))
        copies.append(pltpu.make_async_copy(out.at[m], hbm.at[m], sems.at[m]))
        copies[-1].start()
    for copy in copies:
        copy.wait()


def per_device(counts, links):
    time_len, depth, flat = links.shape[4:]
    sites = time_len * depth
    assert flat == LANES and (time_len, depth) == (4, 4)
    halves = sites // SUB
    vmem = lambda *s: pltpu.VMEM(s + (LANES,), jnp.float32)
    shape = links.shape[:4] + (sites, flat)
    terms = pl.pallas_call(
        functools.partial(force_terms, counts, depth, halves),
        out_shape=pltpu.VMEM((32 * sites, flat), jnp.float32),
        in_specs=[pl.BlockSpec(memory_space=pl.ANY)],
        out_specs=pl.BlockSpec(memory_space=pltpu.VMEM),
        scratch_shapes=[
            vmem(*shape[:-1]),
            vmem(TOTAL),
            vmem(TOTAL),
            vmem(5, 3, 2, 2, 3, SUB),
            vmem(5, 2, 3, 3, SUB),
            vmem(5, 2, 3, 3, SUB),
            pltpu.SemaphoreType.DMA,
            pltpu.SemaphoreType.DMA,
            pltpu.SemaphoreType.DMA((8,)),
        ],
        compiler_params=pltpu.CompilerParams(collective_id=0, has_side_effects=True),
        name="force_terms",
    )(links.reshape(shape))
    out = pl.pallas_call(
        functools.partial(expand, halves),
        out_shape=jax.ShapeDtypeStruct(shape, jnp.float32),
        in_specs=[pl.BlockSpec(memory_space=pltpu.VMEM)],
        out_specs=pl.BlockSpec(memory_space=pl.ANY),
        scratch_shapes=[vmem(*shape[:-1]), pltpu.SemaphoreType.DMA((4,))],
        name="expand",
    )(pltpu.with_memory_space_constraint(terms, pltpu.VMEM))
    return out.reshape(links.shape)


def solution(mesh):
    assert mesh.axis_names == ("gx", "gz", "ta")
    counts = tuple(mesh.shape[a] for a in AXES)
    spec = P(None, None, None, None, "ta", "gz", "gx")
    return jax.shard_map(
        functools.partial(per_device, counts),
        mesh=mesh,
        in_specs=(spec,),
        out_specs=spec,
        check_vma=False,
    )
```

time: 18.1 us -> 17.2 us (0.950)
  Pallas kernels: 18 us -> 17 us
    pallas_call x1, Pallas kernels: 17.2 us -> 16.2 us  [per_device(): pl.pallas_call(functools.partial(force_terms, counts, depth, halves), out...]
where the time goes in v2:
time: 17.2 us; the launch traced here: 17 us
  Pallas kernels  17 us (99%)
    pallas_call x1, Pallas kernels, per_device(): pl.pallas_call(functools.partial(force_terms, counts, depth, halves), out...  16.2 us
    pallas_call x1, Pallas kernels, per_device(): pl.pallas_call(functools.partial(expand, halves), out_shape=jax.ShapeDtyp...  0.86 us

profile of v2, /device:TPU:1, one launch (start us, length us, event | category | flops | bytes accessed | tf_op | source)
XLA Modules:
  0.0 17.0 jit_solution(10061098160085731848)
XLA Ops:
  0.0 16.2 %force_terms.1.acc = f32[512,128]{1,0:T(8,128)S(1)} custom-call(f32[4,2,3,3,16,128]{5,4,3,2,1,0:T(8,128)} %bitcast.2), custom_call_target="tpu_custom_call" | custom-call | tf_op jit(solution)/shard_map/force_terms/pallas_call | solution.py:519
  16.2 0.9 %expand.1 = f32[4,2,3,3,16,128]{5,4,3,2,1,0:T(8,128)} custom-call(f32[512,128]{1,0:T(8,128)S(1)} %force_terms.1.acc), custom_call_target="tpu_custom_call" | custom-call | tf_op jit(solution)/shard_map/expand/pallas_call | solution.py:538

commit v3 on v2

--- a/solution.py
+++ b/solution.py
@@ -263,12 +263,49 @@
         n = sets.index((d, s))
         return complete_rows(lambda part, i, j: face_s[n, q, part, i, j])
 
+    def own_face(d):
+        def get(part, i, j):
+            if d != 2:
+                return pack(d, 0, lambda m, h: load(d, part, i, j, h), True)
+            pair = [shifted(d, load(d, part, i, j, h), h - last[d]) for h in range(halves)]
+            pair = jnp.where(place[d] >= 1, pair[1], pair[0])
+            value = jnp.where(place[d] >= 2, shifted(d, pair, 2), pair)
+            return jnp.where(place[d] >= 4, shifted(d, pair, 4), value)
+
+        return complete_rows(get)
+
+    def step_in_face(d, m, v):
+        if m == 3:
+            return jnp.where(g.xcol == NX - 1, g.lanes(v, NX - 1), g.lanes(v, -1))
+        if m == 2:
+            return g.lanes(v, -NX)
+        if m == 1:
+            return g.rows(v, -1)
+        moved = g.rows(v, -depth)
+        if d == 1:
+            beyond = g.rows(v, depth - 1)
+            return jnp.where(jnp.logical_and(g.zrow == 0, g.row >= depth), beyond, moved)
+        return jnp.where(g.row >= depth, g.lanes(moved, -NX), moved)
+
+    def over_face(d, s, own):
+        def get(part, i, j):
+            value, before = None, None
+            for k, (m, h) in enumerate(LAYOUT[d][s]):
+                if m == before:
+                    continue
+                x = step_in_face(d, m, own[part][i][j])
+                value = x if value is None else jnp.where(place[d] >= k, x, value)
+                before = m
+            return value
+
+        return complete_rows(get)
+
     def send_side(d):
-        own = packed(d, 0, lambda m, h, *c: load(d, *c, h), True)
+        own = own_face(d)
         for s in range(len(LAYOUT[d])):
             n = sets.index((d, s))
             side = packed(d, s, lambda m, h, *c: load(m, *c, h), True)
-            over = packed(d, s, lambda m, h, *c: rolled(d, m, h, *c), True)
+            over = over_face(d, s, own)
             b = product(own, side, left_h=True)
             mask = open_mask(d, s)
             put("g", d, s, [
@@ -281,6 +318,9 @@
             for q, value in enumerate((own, side, over)):
                 save(face_s, (n, q), value)
             save(b_s, (n,), b)
+
+    def send_face(d):
+        for s in range(len(LAYOUT[d])):
             put("x", d, s, [
                 [
                     [pack(d, s, lambda m, h: load(m, p, i, j, h), False) for j in range(3)]
@@ -330,13 +370,17 @@
 
     everything_in = pltpu.make_async_copy(hbm, u, load_sem)
     everything_in.wait()
-    for d in (1, 0, 2):
-        send_side(d)
     for d, n in DIAGONALS:
         pack_edges(d, n)
+    for d in (1, 0):
+        send_side(d)
+        send_face(d)
+    send_face(2)
     pl.semaphore_wait(barrier, len(partners))
-    for copy in [opens[1], faces[1]] + edges[2:] + [opens[0], faces[0], opens[2], faces[2]] + edges[:2]:
+    for copy in edges[2:] + [opens[1], faces[1]] + edges[:2] + [opens[0], faces[0], faces[2]]:
         copy.start()
+    send_side(2)
+    opens[2].start()
 
     seen, pending = set(), {}
 

time: 17.2 us -> 16.7 us (0.971)
  Pallas kernels: 17 us -> 16.5 us
    pallas_call x1, Pallas kernels: 16.2 us -> 15.7 us  [per_device(): pl.pallas_call(functools.partial(force_terms, counts, depth, halves), out...]
where the time goes in v3:
time: 16.7 us; the launch traced here: 16.5 us
  Pallas kernels  16.5 us (99%)
    pallas_call x1, Pallas kernels, per_device(): pl.pallas_call(functools.partial(force_terms, counts, depth, halves), out...  15.7 us
    pallas_call x1, Pallas kernels, per_device(): pl.pallas_call(functools.partial(expand, halves), out_shape=jax.ShapeDtyp...  0.86 us

profile of v3, /device:TPU:1, one launch (start us, length us, event | category | flops | bytes accessed | tf_op | source)
XLA Modules:
  0.0 16.5 jit_solution(13229630332526217614)
XLA Ops:
  0.0 15.7 %force_terms.1.acc = f32[512,128]{1,0:T(8,128)S(1)} custom-call(f32[4,2,3,3,16,128]{5,4,3,2,1,0:T(8,128)} %bitcast.2), custom_call_target="tpu_custom_call" | custom-call | tf_op jit(solution)/shard_map/force_terms/pallas_call | solution.py:563
  15.7 0.9 %expand.1 = f32[4,2,3,3,16,128]{5,4,3,2,1,0:T(8,128)} custom-call(f32[512,128]{1,0:T(8,128)S(1)} %force_terms.1.acc), custom_call_target="tpu_custom_call" | custom-call | tf_op jit(solution)/shard_map/expand/pallas_call | solution.py:582

commit v4 on v3

--- a/solution.py
+++ b/solution.py
@@ -114,7 +114,7 @@
 
 
 def force_terms(
-    counts, depth, halves, hbm, acc, u, out_s, in_s, face_s, b_s, pre_s, load_sem, send, recv,
+    counts, depth, halves, hbm, acc, u, out_s, in_s, face_s, b_s, pre_s, load_sem, send, recv, met,
 ):
     g = Lattice(depth)
     me = [lax.axis_index(a) for a in AXES]
@@ -130,15 +130,15 @@
         return (by["gx"], by["gz"], by["ta"])
 
     loads = [
-        pltpu.make_async_copy(hbm.at[m, part], u.at[m, part], load_sem)
+        pltpu.make_async_copy(hbm.at[m, part, i], u.at[m, part, i], load_sem)
         for m in range(4)
         for part in range(2)
+        for i in range(3)
     ]
     for copy in loads:
         copy.start()
     barrier = pltpu.get_barrier_semaphore()
     partners = [device((i, step)) for i in (1, 0, 2) for step in (1, -1)]
-    partners += [device((d, 1), (n, -1)) for d, n in DIAGONALS]
     for where in partners:
         pl.semaphore_signal(barrier, inc=1, device_id=where, device_id_type=pl.DeviceIdType.MESH)
 
@@ -377,7 +377,9 @@
         send_face(d)
     send_face(2)
     pl.semaphore_wait(barrier, len(partners))
-    for copy in edges[2:] + [opens[1], faces[1]] + edges[:2] + [opens[0], faces[0], faces[2]]:
+    for where in partners[2:]:
+        pl.semaphore_signal(met, inc=1, device_id=where, device_id_type=pl.DeviceIdType.MESH)
+    for copy in [opens[1], faces[1], opens[0], faces[0], faces[2]]:
         copy.start()
     send_side(2)
     opens[2].start()
@@ -503,7 +505,11 @@
                     add(m, c, half(d, h, False), jnp.where(bottom(d), shifted(d, q[c], -k), 0.0))
         flush()
 
-    for pair in PLANES:
+    for n, pair in enumerate(PLANES):
+        if n == 3:
+            pl.semaphore_wait(met, len(partners) - 2)
+            for copy in edges[2:] + edges[:2]:
+                copy.start()
         for h in range(halves):
             inner(*pair, h)
         flush()
@@ -527,8 +533,7 @@
     everything.wait_send()
 
 
-def expand(halves, acc, hbm, out, sems):
-    copies = []
+def expand(halves, acc, hbm, out, sem):
     for m in range(4):
         for h in range(halves):
             rows = [((m * 8 + c) * halves + h) * SUB for c in range(8)]
@@ -547,10 +552,10 @@
             put(1, 0, 0, f[6])
             put(1, 1, 1, f[7])
             put(1, 2, 2, -(f[6] + f[7]))
-        copies.append(pltpu.make_async_copy(out.at[m], hbm.at[m], sems.at[m]))
-        copies[-1].start()
-    for copy in copies:
-        copy.wait()
+        for part in range(2):
+            for i in range(3):
+                pltpu.make_async_copy(out.at[m, part, i], hbm.at[m, part, i], sem).start()
+    pltpu.make_async_copy(out, hbm, sem).wait()
 
 
 def per_device(counts, links):
@@ -575,6 +580,7 @@
             pltpu.SemaphoreType.DMA,
             pltpu.SemaphoreType.DMA,
             pltpu.SemaphoreType.DMA((8,)),
+            pltpu.SemaphoreType.REGULAR,
         ],
         compiler_params=pltpu.CompilerParams(collective_id=0, has_side_effects=True),
         name="force_terms",
@@ -584,7 +590,7 @@
         out_shape=jax.ShapeDtypeStruct(shape, jnp.float32),
         in_specs=[pl.BlockSpec(memory_space=pltpu.VMEM)],
         out_specs=pl.BlockSpec(memory_space=pl.ANY),
-        scratch_shapes=[vmem(*shape[:-1]), pltpu.SemaphoreType.DMA((4,))],
+        scratch_shapes=[vmem(*shape[:-1]), pltpu.SemaphoreType.DMA],
         name="expand",
     )(pltpu.with_memory_space_constraint(terms, pltpu.VMEM))
     return out.reshape(links.shape)

time: 16.7 us -> 17.4 us (1.042)
  Pallas kernels: 16.5 us -> 17.2 us
    pallas_call x1, Pallas kernels: 15.7 us -> 16.4 us  [per_device(): pl.pallas_call(functools.partial(force_terms, counts, depth, halves), out...]
where the time goes in v4:
time: 17.4 us; the launch traced here: 17.2 us
  Pallas kernels  17.2 us (99%)
    pallas_call x1, Pallas kernels, per_device(): pl.pallas_call(functools.partial(force_terms, counts, depth, halves), out...  16.4 us
    pallas_call x1, Pallas kernels, per_device(): pl.pallas_call(functools.partial(expand, halves), out_shape=jax.ShapeDtyp...  0.81 us

profile of v4, /device:TPU:1, one launch (start us, length us, event | category | flops | bytes accessed | tf_op | source)
XLA Modules:
  0.0 17.2 jit_solution(16459735187214782348)
XLA Ops:
  0.0 16.4 %force_terms.1.acc = f32[512,128]{1,0:T(8,128)S(1)} custom-call(f32[4,2,3,3,16,128]{5,4,3,2,1,0:T(8,128)} %bitcast.2), custom_call_target="tpu_custom_call" | custom-call | tf_op jit(solution)/shard_map/force_terms/pallas_call | solution.py:568
  16.4 0.8 %expand.1 = f32[4,2,3,3,16,128]{5,4,3,2,1,0:T(8,128)} custom-call(f32[512,128]{1,0:T(8,128)S(1)} %force_terms.1.acc), custom_call_target="tpu_custom_call" | custom-call | tf_op jit(solution)/shard_map/expand/pallas_call | solution.py:588

commit v5 on v4

--- a/solution.py
+++ b/solution.py
@@ -94,7 +94,15 @@
 
 
 PLANES = ((0, 1), (0, 2), (0, 3), (1, 2), (1, 3), (2, 3))
-DIAGONALS = ((0, 2), (2, 0), (0, 1), (1, 0), (1, 2), (2, 1))
+DIAGONALS = ((0, 1), (1, 0), (1, 2), (2, 1), (0, 2), (2, 0))
+LEGS = (
+    ((0, 1), (1, -1)),
+    ((0, -1), (1, 1)),
+    ((2, -1), (1, 1)),
+    ((2, 1), (1, -1)),
+    ((2, -1), (0, 1)),
+    ((2, 1), (0, -1)),
+)
 LAYOUT = (
     (((1, 0), (2, 0)), ((3, 0),)),
     (((0, 0), (0, 1), (2, 0), (2, 1)), ((3, 0), (3, 1))),
@@ -114,7 +122,8 @@
 
 
 def force_terms(
-    counts, depth, halves, hbm, acc, u, out_s, in_s, face_s, b_s, pre_s, load_sem, send, recv, met,
+    counts, depth, halves, hbm, acc, u, out_s, in_s, relay_s, face_s, b_s, pre_s,
+    load_sem, send, recv, passed,
 ):
     g = Lattice(depth)
     me = [lax.axis_index(a) for a in AXES]
@@ -151,12 +160,31 @@
 
     faces = [remote(offset("x", d), ROWS[d], d, device((d, -1))) for d in range(3)]
     opens = [remote(offset("g", d), ROWS[d], 3 + d, device((d, 1))) for d in range(3)]
-    edges = [
-        remote(offset("e", k), EDGE, 6 if k < 2 else 7, device((d, 1), (n, -1)))
-        for k, (d, n) in enumerate(DIAGONALS)
-    ]
-    near_edges = remote(offset("e", 0), 2 * EDGE, 6, partners[0])
-    far_edges = remote(offset("e", 2), 4 * EDGE, 7, partners[0])
+    first_legs, second_legs = [], []
+    for k, (leg, then) in enumerate(LEGS):
+        span = slice(k * EDGE, (k + 1) * EDGE)
+        at = slice(offset("e", k), offset("e", k + 1))
+        first_legs.append(
+            pltpu.make_async_remote_copy(
+                src_ref=out_s.at[at], dst_ref=relay_s.at[span], send_sem=send, recv_sem=recv.at[6],
+                device_id=device(leg), device_id_type=pl.DeviceIdType.MESH,
+            )
+        )
+        second_legs.append(
+            pltpu.make_async_remote_copy(
+                src_ref=relay_s.at[span], dst_ref=in_s.at[at], send_sem=passed, recv_sem=recv.at[7],
+                device_id=device(then), device_id_type=pl.DeviceIdType.MESH,
+            )
+        )
+    edge_rows = slice(offset("e", 0), TOTAL)
+    relayed = pltpu.make_async_remote_copy(
+        src_ref=relay_s, dst_ref=relay_s, send_sem=passed, recv_sem=recv.at[6],
+        device_id=partners[0], device_id_type=pl.DeviceIdType.MESH,
+    )
+    edges = pltpu.make_async_remote_copy(
+        src_ref=relay_s, dst_ref=in_s.at[edge_rows], send_sem=passed, recv_sem=recv.at[7],
+        device_id=partners[0], device_id_type=pl.DeviceIdType.MESH,
+    )
     everything = remote(0, TOTAL, 0, partners[0])
 
     def load(m, part, i, j, h):
@@ -377,12 +405,13 @@
         send_face(d)
     send_face(2)
     pl.semaphore_wait(barrier, len(partners))
-    for where in partners[2:]:
-        pl.semaphore_signal(met, inc=1, device_id=where, device_id_type=pl.DeviceIdType.MESH)
-    for copy in [opens[1], faces[1], opens[0], faces[0], faces[2]]:
+    for copy in first_legs + [opens[1], faces[1], opens[0], faces[0], faces[2]]:
         copy.start()
     send_side(2)
     opens[2].start()
+    relayed.wait_recv()
+    for copy in second_legs:
+        copy.start()
 
     seen, pending = set(), {}
 
@@ -505,11 +534,7 @@
                     add(m, c, half(d, h, False), jnp.where(bottom(d), shifted(d, q[c], -k), 0.0))
         flush()
 
-    for n, pair in enumerate(PLANES):
-        if n == 3:
-            pl.semaphore_wait(met, len(partners) - 2)
-            for copy in edges[2:] + edges[:2]:
-                copy.start()
+    for pair in PLANES:
         for h in range(halves):
             inner(*pair, h)
         flush()
@@ -519,17 +544,15 @@
     faces[0].wait_recv()
     face_terms(0, (2,))
     corners(1, (0, 2))
-    near_edges.wait_recv()
-    far_edges.wait_recv()
+    faces[1].wait_recv()
+    face_terms(1, (0, 2))
+    edges.wait_recv()
     for d in (2, 0, 1):
         prepare(d)
-    for d in (2, 0):
+    for d in (2, 0, 1):
         opens[d].wait_recv()
         close(d)
-    faces[1].wait_recv()
-    face_terms(1, (0, 2))
-    opens[1].wait_recv()
-    close(1)
+    relayed.wait_send()
     everything.wait_send()
 
 
@@ -574,13 +597,14 @@
             vmem(*shape[:-1]),
             vmem(TOTAL),
             vmem(TOTAL),
+            vmem(len(LEGS) * EDGE),
             vmem(5, 3, 2, 2, 3, SUB),
             vmem(5, 2, 3, 3, SUB),
             vmem(5, 2, 3, 3, SUB),
             pltpu.SemaphoreType.DMA,
             pltpu.SemaphoreType.DMA,
             pltpu.SemaphoreType.DMA((8,)),
-            pltpu.SemaphoreType.REGULAR,
+            pltpu.SemaphoreType.DMA,
         ],
         compiler_params=pltpu.CompilerParams(collective_id=0, has_side_effects=True),
         name="force_terms",

time: 17.4 us -> 18.8 us (1.080)
  Pallas kernels: 17.2 us -> 18.6 us
    pallas_call x1, Pallas kernels: 16.4 us -> 17.8 us  [per_device(): pl.pallas_call(functools.partial(force_terms, counts, depth, halves), out...]
where the time goes in v5:
time: 18.8 us; the launch traced here: 18.6 us
  Pallas kernels  18.6 us (99%)
    pallas_call x1, Pallas kernels, per_device(): pl.pallas_call(functools.partial(force_terms, counts, depth, halves), out...  17.8 us
    pallas_call x1, Pallas kernels, per_device(): pl.pallas_call(functools.partial(expand, halves), out_shape=jax.ShapeDtyp...  0.81 us

profile of v5, /device:TPU:1, one launch (start us, length us, event | category | flops | bytes accessed | tf_op | source)
XLA Modules:
  0.0 18.6 jit_solution(40312606018866626)
XLA Ops:
  0.0 17.8 %force_terms.1.acc = f32[512,128]{1,0:T(8,128)S(1)} custom-call(f32[4,2,3,3,16,128]{5,4,3,2,1,0:T(8,128)} %bitcast.2), custom_call_target="tpu_custom_call" | custom-call | tf_op jit(solution)/shard_map/force_terms/pallas_call | solution.py:591
  17.8 0.8 %expand.1 = f32[4,2,3,3,16,128]{5,4,3,2,1,0:T(8,128)} custom-call(f32[512,128]{1,0:T(8,128)S(1)} %force_terms.1.acc), custom_call_target="tpu_custom_call" | custom-call | tf_op jit(solution)/shard_map/expand/pallas_call | solution.py:612

commit v6 on v4

--- a/solution.py
+++ b/solution.py
@@ -101,12 +101,12 @@
     (((0, 0), (0, 1), (1, 0), (1, 1), (3, 0), (3, 1)),),
 )
 ROWS = (144, 144, 96)
-EDGE = 2 * SUB
+EDGES = (8, 8, 16, 16, 8, 8)
 
 
 def offset(kind, d):
     if kind == "e":
-        return 2 * sum(ROWS) + d * EDGE
+        return 2 * sum(ROWS) + sum(EDGES[:d])
     return (sum(ROWS) if kind == "g" else 0) + sum(ROWS[:d])
 
 
@@ -114,7 +114,7 @@
 
 
 def force_terms(
-    counts, depth, halves, hbm, acc, u, out_s, in_s, face_s, b_s, pre_s, load_sem, send, recv, met,
+    counts, depth, halves, hbm, acc, u, out_s, in_s, face_s, b_s, pre_s, load_sem, send, recv,
 ):
     g = Lattice(depth)
     me = [lax.axis_index(a) for a in AXES]
@@ -139,7 +139,8 @@
         copy.start()
     barrier = pltpu.get_barrier_semaphore()
     partners = [device((i, step)) for i in (1, 0, 2) for step in (1, -1)]
-    for where in partners:
+    partners += [device((d, 1), (n, -1)) for d, n in DIAGONALS]
+    for where in partners[6:] + partners[:6]:
         pl.semaphore_signal(barrier, inc=1, device_id=where, device_id_type=pl.DeviceIdType.MESH)
 
     def remote(start, rows, slot, where):
@@ -152,11 +153,10 @@
     faces = [remote(offset("x", d), ROWS[d], d, device((d, -1))) for d in range(3)]
     opens = [remote(offset("g", d), ROWS[d], 3 + d, device((d, 1))) for d in range(3)]
     edges = [
-        remote(offset("e", k), EDGE, 6 if k < 2 else 7, device((d, 1), (n, -1)))
+        remote(offset("e", k), EDGES[k], 6, device((d, 1), (n, -1)))
         for k, (d, n) in enumerate(DIAGONALS)
     ]
-    near_edges = remote(offset("e", 0), 2 * EDGE, 6, partners[0])
-    far_edges = remote(offset("e", 2), 4 * EDGE, 7, partners[0])
+    all_edges = remote(offset("e", 0), sum(EDGES), 6, partners[0])
     everything = remote(0, TOTAL, 0, partners[0])
 
     def load(m, part, i, j, h):
@@ -331,42 +331,58 @@
 
     def pack_edges(d, n):
         r0 = offset("e", DIAGONALS.index((d, n)))
-        for c0 in range(0, 12, SUB):
-            value = None
-            for k in range(min(SUB, 12 - c0)):
-                c = comps[c0 + k]
-                if 2 not in (d, n):
-                    v = load(d, *c, halves - 1 if d == 0 else 0)
+        if 2 not in (d, n):
+            for c0 in range(0, 12, SUB):
+                value = None
+                for k in range(min(SUB, 12 - c0)):
+                    v = load(d, *comps[c0 + k], halves - 1 if d == 0 else 0)
                     x = g.rows(v, k - depth if d == 0 else k - (depth - 1))
                     value = x if value is None else jnp.where(g.row >= k, x, value)
-                    continue
-                if 0 in (d, n):
-                    v = load(d, *c, halves - 1 if d == 0 else 0)
-                else:
-                    at = depth - 1 if d == 1 else 0
-                    step = -1 if d == 1 else 1
-                    v = load(d, *c, 0)
-                    for h in range(1, halves):
-                        v = jnp.where(g.zrow == at + step * h, g.rows(load(d, *c, h), step * h), v)
-                x = g.lanes(v, NX * (k + (1 if d == 2 else 0)))
-                value = x if value is None else jnp.where(g.lane >= NX * k, x, value)
-            out_s[r0 + c0 : r0 + c0 + SUB, :] = value
+                out_s[r0 + c0 : r0 + c0 + SUB, :] = value
+            return
+        value = None
+        for k in range(g.ygroups):
+            v = dense_rows(d, n, comps[k])
+            if k + g.ygroups < 12:
+                w = dense_rows(d, n, comps[k + g.ygroups])
+                step, mask = spare(d, n)
+                v = jnp.where(mask, v, g.rows(w, step))
+            x = g.lanes(v, NX * (k + (1 if d == 2 else 0)))
+            value = x if value is None else jnp.where(g.lane >= NX * k, x, value)
+        out_s[r0 : r0 + SUB, :] = value
+
+    def spare(d, n):
+        if (d, n) == (0, 2):
+            return depth, g.row >= depth
+        if (d, n) == (2, 0):
+            return depth, g.row < depth
+        return (-2, g.zrow >= 2) if d == 1 else (2, g.zrow < 2)
+
+    def dense_rows(d, n, c):
+        if 0 in (d, n):
+            return load(d, *c, halves - 1 if d == 0 else 0)
+        at = depth - 1 if d == 1 else 0
+        step = -1 if d == 1 else 1
+        v = load(d, *c, 0)
+        for h in range(1, halves):
+            v = jnp.where(g.zrow == at + step * h, g.rows(load(d, *c, h), step * h), v)
+        return v
 
     def edge(d, n, h, part, i, j):
         c = part * 6 + i * 3 + j
-        r = offset("e", DIAGONALS.index((d, n))) + c // SUB * SUB
-        v = in_s[r : r + SUB, :]
-        k = c % SUB
-        if (d, n) == (0, 1):
-            return g.rows(v, depth - 1 - k)
-        if (d, n) == (1, 0):
-            return g.rows(v, SUB - depth - k)
-        v = g.lanes(v, NX * ((0 if d == 2 else g.ygroups - 1) - k))
+        r = offset("e", DIAGONALS.index((d, n)))
+        if 2 not in (d, n):
+            v = in_s[r + c // SUB * SUB : r + c // SUB * SUB + SUB, :]
+            k = c % SUB
+            return g.rows(v, depth - 1 - k if d == 0 else SUB - depth - k)
+        k, back = c % g.ygroups, c >= g.ygroups
+        v = g.lanes(in_s[r : r + SUB, :], NX * ((0 if d == 2 else g.ygroups - 1) - k))
+        step = -spare(d, n)[0] if back else 0
         if (d, n) == (0, 2):
-            return g.rows(v, -(SUB - depth))
+            return g.rows(v, step - (SUB - depth))
         if (d, n) == (2, 0):
-            return g.rows(v, SUB - depth)
-        return g.rows(v, 1 - depth + h if d == 1 else depth - 1 - h)
+            return g.rows(v, step + SUB - depth)
+        return g.rows(v, step + (1 - depth + h if d == 1 else depth - 1 - h))
 
     everything_in = pltpu.make_async_copy(hbm, u, load_sem)
     everything_in.wait()
@@ -377,11 +393,10 @@
         send_face(d)
     send_face(2)
     pl.semaphore_wait(barrier, len(partners))
-    for where in partners[2:]:
-        pl.semaphore_signal(met, inc=1, device_id=where, device_id_type=pl.DeviceIdType.MESH)
-    for copy in [opens[1], faces[1], opens[0], faces[0], faces[2]]:
+    for copy in edges[2:] + [opens[1], faces[1]] + edges[:2] + [opens[0], faces[0]]:
         copy.start()
     send_side(2)
+    faces[2].start()
     opens[2].start()
 
     seen, pending = set(), {}
@@ -505,11 +520,7 @@
                     add(m, c, half(d, h, False), jnp.where(bottom(d), shifted(d, q[c], -k), 0.0))
         flush()
 
-    for n, pair in enumerate(PLANES):
-        if n == 3:
-            pl.semaphore_wait(met, len(partners) - 2)
-            for copy in edges[2:] + edges[:2]:
-                copy.start()
+    for pair in PLANES:
         for h in range(halves):
             inner(*pair, h)
         flush()
@@ -519,8 +530,7 @@
     faces[0].wait_recv()
     face_terms(0, (2,))
     corners(1, (0, 2))
-    near_edges.wait_recv()
-    far_edges.wait_recv()
+    all_edges.wait_recv()
     for d in (2, 0, 1):
         prepare(d)
     for d in (2, 0):
@@ -579,8 +589,7 @@
             vmem(5, 2, 3, 3, SUB),
             pltpu.SemaphoreType.DMA,
             pltpu.SemaphoreType.DMA,
-            pltpu.SemaphoreType.DMA((8,)),
-            pltpu.SemaphoreType.REGULAR,
+            pltpu.SemaphoreType.DMA((7,)),
         ],
         compiler_params=pltpu.CompilerParams(collective_id=0, has_side_effects=True),
         name="force_terms",

time: 17.4 us -> 16.7 us (0.960)
  Pallas kernels: 17.2 us -> 16.6 us
    pallas_call x1, Pallas kernels: 16.4 us -> 15.7 us  [per_device(): pl.pallas_call(functools.partial(force_terms, counts, depth, halves), out...]
where the time goes in v6:
time: 16.7 us; the launch traced here: 16.6 us
  Pallas kernels  16.6 us (99%)
    pallas_call x1, Pallas kernels, per_device(): pl.pallas_call(functools.partial(force_terms, counts, depth, halves), out...  15.7 us
    pallas_call x1, Pallas kernels, per_device(): pl.pallas_call(functools.partial(expand, halves), out_shape=jax.ShapeDtyp...  0.81 us

profile of v6, /device:TPU:1, one launch (start us, length us, event | category | flops | bytes accessed | tf_op | source)
XLA Modules:
  0.0 16.6 jit_solution(1093548517601304529)
XLA Ops:
  0.0 15.7 %force_terms.1.acc = f32[512,128]{1,0:T(8,128)S(1)} custom-call(f32[4,2,3,3,16,128]{5,4,3,2,1,0:T(8,128)} %bitcast.2), custom_call_target="tpu_custom_call" | custom-call | tf_op jit(solution)/shard_map/force_terms/pallas_call | solution.py:578
  15.8 0.8 %expand.1 = f32[4,2,3,3,16,128]{5,4,3,2,1,0:T(8,128)} custom-call(f32[512,128]{1,0:T(8,128)S(1)} %force_terms.1.acc), custom_call_target="tpu_custom_call" | custom-call | tf_op jit(solution)/shard_map/expand/pallas_call | solution.py:597

commit v7 on v6

--- a/solution.py
+++ b/solution.py
@@ -114,7 +114,7 @@
 
 
 def force_terms(
-    counts, depth, halves, hbm, acc, u, out_s, in_s, face_s, b_s, pre_s, load_sem, send, recv,
+    counts, depth, halves, hbm, acc, u, out_s, in_s, face_s, b_s, pre_s, load_sem, send, recv, met,
 ):
     g = Lattice(depth)
     me = [lax.axis_index(a) for a in AXES]
@@ -139,7 +139,7 @@
         copy.start()
     barrier = pltpu.get_barrier_semaphore()
     partners = [device((i, step)) for i in (1, 0, 2) for step in (1, -1)]
-    partners += [device((d, 1), (n, -1)) for d, n in DIAGONALS]
+    partners += [device((d, 1), (n, -1)) for d, n in DIAGONALS[2:]]
     for where in partners[6:] + partners[:6]:
         pl.semaphore_signal(barrier, inc=1, device_id=where, device_id_type=pl.DeviceIdType.MESH)
 
@@ -393,7 +393,9 @@
         send_face(d)
     send_face(2)
     pl.semaphore_wait(barrier, len(partners))
-    for copy in edges[2:] + [opens[1], faces[1]] + edges[:2] + [opens[0], faces[0]]:
+    for where in partners[4:6]:
+        pl.semaphore_signal(met, inc=1, device_id=where, device_id_type=pl.DeviceIdType.MESH)
+    for copy in edges[2:] + [opens[1], faces[1], opens[0], faces[0]]:
         copy.start()
     send_side(2)
     faces[2].start()
@@ -520,7 +522,11 @@
                     add(m, c, half(d, h, False), jnp.where(bottom(d), shifted(d, q[c], -k), 0.0))
         flush()
 
-    for pair in PLANES:
+    for n, pair in enumerate(PLANES):
+        if n == 2:
+            pl.semaphore_wait(met, 2)
+            for copy in edges[:2]:
+                copy.start()
         for h in range(halves):
             inner(*pair, h)
         flush()
@@ -530,16 +536,15 @@
     faces[0].wait_recv()
     face_terms(0, (2,))
     corners(1, (0, 2))
+    faces[1].wait_recv()
+    face_terms(1, (0, 2))
     all_edges.wait_recv()
     for d in (2, 0, 1):
         prepare(d)
-    for d in (2, 0):
+    for d in (2, 0, 1):
         opens[d].wait_recv()
+    for d in (2, 0, 1):
         close(d)
-    faces[1].wait_recv()
-    face_terms(1, (0, 2))
-    opens[1].wait_recv()
-    close(1)
     everything.wait_send()
 
 
@@ -590,6 +595,7 @@
             pltpu.SemaphoreType.DMA,
             pltpu.SemaphoreType.DMA,
             pltpu.SemaphoreType.DMA((7,)),
+            pltpu.SemaphoreType.REGULAR,
         ],
         compiler_params=pltpu.CompilerParams(collective_id=0, has_side_effects=True),
         name="force_terms",

time: 16.7 us -> 16.4 us (0.982)
  Pallas kernels: 16.6 us -> 16.2 us
    pallas_call x1, Pallas kernels: 15.7 us -> 15.4 us  [per_device(): pl.pallas_call(functools.partial(force_terms, counts, depth, halves), out...]
where the time goes in v7:
time: 16.4 us; the launch traced here: 16.2 us
  Pallas kernels  16.2 us (99%)
    pallas_call x1, Pallas kernels, per_device(): pl.pallas_call(functools.partial(force_terms, counts, depth, halves), out...  15.4 us
    pallas_call x1, Pallas kernels, per_device(): pl.pallas_call(functools.partial(expand, halves), out_shape=jax.ShapeDtyp...  0.81 us

profile of v7, /device:TPU:1, one launch (start us, length us, event | category | flops | bytes accessed | tf_op | source)
XLA Modules:
  0.0 16.2 jit_solution(13889555382825794308)
XLA Ops:
  0.0 15.4 %force_terms.1.acc = f32[512,128]{1,0:T(8,128)S(1)} custom-call(f32[4,2,3,3,16,128]{5,4,3,2,1,0:T(8,128)} %bitcast.2), custom_call_target="tpu_custom_call" | custom-call | tf_op jit(solution)/shard_map/force_terms/pallas_call | solution.py:583
  15.4 0.8 %expand.1 = f32[4,2,3,3,16,128]{5,4,3,2,1,0:T(8,128)} custom-call(f32[512,128]{1,0:T(8,128)S(1)} %force_terms.1.acc), custom_call_target="tpu_custom_call" | custom-call | tf_op jit(solution)/shard_map/expand/pallas_call | solution.py:603

commit v8 on v7

--- a/solution.py
+++ b/solution.py
@@ -139,7 +139,7 @@
         copy.start()
     barrier = pltpu.get_barrier_semaphore()
     partners = [device((i, step)) for i in (1, 0, 2) for step in (1, -1)]
-    partners += [device((d, 1), (n, -1)) for d, n in DIAGONALS[2:]]
+    partners += [device((d, 1), (n, -1)) for d, n in DIAGONALS[2:]] + [device((0, -1), (2, 1))]
     for where in partners[6:] + partners[:6]:
         pl.semaphore_signal(barrier, inc=1, device_id=where, device_id_type=pl.DeviceIdType.MESH)
 
@@ -393,9 +393,8 @@
         send_face(d)
     send_face(2)
     pl.semaphore_wait(barrier, len(partners))
-    for where in partners[4:6]:
-        pl.semaphore_signal(met, inc=1, device_id=where, device_id_type=pl.DeviceIdType.MESH)
-    for copy in edges[2:] + [opens[1], faces[1], opens[0], faces[0]]:
+    pl.semaphore_signal(met, inc=1, device_id=partners[5], device_id_type=pl.DeviceIdType.MESH)
+    for copy in edges[2:] + edges[:1] + [opens[1], faces[1], opens[0], faces[0]]:
         copy.start()
     send_side(2)
     faces[2].start()
@@ -524,9 +523,8 @@
 
     for n, pair in enumerate(PLANES):
         if n == 2:
-            pl.semaphore_wait(met, 2)
-            for copy in edges[:2]:
-                copy.start()
+            pl.semaphore_wait(met, 1)
+            edges[1].start()
         for h in range(halves):
             inner(*pair, h)
         flush()

time: 16.4 us -> 15.9 us (0.970)
  Pallas kernels: 16.2 us -> 15.7 us
    pallas_call x1, Pallas kernels: 15.4 us -> 14.9 us  [per_device(): pl.pallas_call(functools.partial(force_terms, counts, depth, halves), out...]
where the time goes in v8:
time: 15.9 us; the launch traced here: 15.7 us
  Pallas kernels  15.7 us (99%)
    pallas_call x1, Pallas kernels, per_device(): pl.pallas_call(functools.partial(force_terms, counts, depth, halves), out...  14.9 us
    pallas_call x1, Pallas kernels, per_device(): pl.pallas_call(functools.partial(expand, halves), out_shape=jax.ShapeDtyp...  0.81 us

profile of v8, /device:TPU:1, one launch (start us, length us, event | category | flops | bytes accessed | tf_op | source)
XLA Modules:
  0.0 15.7 jit_solution(10471214106871577636)
XLA Ops:
  0.0 14.9 %force_terms.1.acc = f32[512,128]{1,0:T(8,128)S(1)} custom-call(f32[4,2,3,3,16,128]{5,4,3,2,1,0:T(8,128)} %bitcast.2), custom_call_target="tpu_custom_call" | custom-call | tf_op jit(solution)/shard_map/force_terms/pallas_call | solution.py:581
  14.9 0.8 %expand.1 = f32[4,2,3,3,16,128]{5,4,3,2,1,0:T(8,128)} custom-call(f32[512,128]{1,0:T(8,128)S(1)} %force_terms.1.acc), custom_call_target="tpu_custom_call" | custom-call | tf_op jit(solution)/shard_map/expand/pallas_call | solution.py:601

commit v9 on v8

--- a/solution.py
+++ b/solution.py
@@ -114,7 +114,7 @@
 
 
 def force_terms(
-    counts, depth, halves, hbm, acc, u, out_s, in_s, face_s, b_s, pre_s, load_sem, send, recv, met,
+    counts, depth, halves, hbm, acc, u, out_s, in_s, face_s, b_s, pre_s, load_sem, send, recv, met, met_t, met_z,
 ):
     g = Lattice(depth)
     me = [lax.axis_index(a) for a in AXES]
@@ -138,10 +138,35 @@
     for copy in loads:
         copy.start()
     barrier = pltpu.get_barrier_semaphore()
-    partners = [device((i, step)) for i in (1, 0, 2) for step in (1, -1)]
-    partners += [device((d, 1), (n, -1)) for d, n in DIAGONALS[2:]] + [device((0, -1), (2, 1))]
-    for where in partners[6:] + partners[:6]:
-        pl.semaphore_signal(barrier, inc=1, device_id=where, device_id_type=pl.DeviceIdType.MESH)
+    first_t, last_t = me[0] == 0, me[0] == counts[0] - 1
+    first_z, last_z = me[1] == 0, me[1] == counts[1] - 1
+    more_t, more_z = jnp.logical_not(last_t), jnp.logical_not(last_z)
+    rest_t, rest_z = jnp.logical_not(first_t), jnp.logical_not(first_z)
+    one = lambda flag: jnp.where(flag, 1, 0)
+
+    def signal(semaphore, *steps):
+        pl.semaphore_signal(
+            semaphore, inc=1, device_id=device(*steps), device_id_type=pl.DeviceIdType.MESH
+        )
+
+    for steps in (((1, -1),), ((2, 1), (1, -1)), ((0, -1), (2, 1)), ((0, -1),), ((2, 1),), ((2, -1),)):
+        signal(barrier, *steps)
+
+    @pl.when(more_z)
+    def _():
+        signal(barrier, (1, 1))
+        signal(barrier, (1, 1), (2, -1))
+
+    @pl.when(jnp.logical_or(more_z, first_t))
+    def _():
+        signal(barrier, (1, 1), (0, -1))
+
+    @pl.when(more_t)
+    def _():
+        signal(barrier, (0, 1))
+        signal(barrier, (0, 1), (1, -1))
+
+    expected = 11 - 2 * one(first_t) - 2 * one(first_z) - one(jnp.logical_and(first_z, more_t))
 
     def remote(start, rows, slot, where):
         span = slice(start, start + rows)
@@ -156,8 +181,8 @@
         remote(offset("e", k), EDGES[k], 6, device((d, 1), (n, -1)))
         for k, (d, n) in enumerate(DIAGONALS)
     ]
-    all_edges = remote(offset("e", 0), sum(EDGES), 6, partners[0])
-    everything = remote(0, TOTAL, 0, partners[0])
+    all_edges = remote(offset("e", 0), sum(EDGES), 6, device((1, 1)))
+    everything = remote(0, TOTAL, 0, device((1, 1)))
 
     def load(m, part, i, j, h):
         return u[m, part, i, j, h * SUB : (h + 1) * SUB, :]
@@ -392,10 +417,33 @@
         send_side(d)
         send_face(d)
     send_face(2)
-    pl.semaphore_wait(barrier, len(partners))
-    pl.semaphore_signal(met, inc=1, device_id=partners[5], device_id_type=pl.DeviceIdType.MESH)
-    for copy in edges[2:] + edges[:1] + [opens[1], faces[1], opens[0], faces[0]]:
+    pl.semaphore_wait(barrier, expected)
+    for copy in [edges[4], edges[0], opens[1], opens[0]]:
         copy.start()
+    signal(met, (2, -1))
+
+    @pl.when(last_t)
+    def _():
+        signal(met_t, (0, 1))
+
+    @pl.when(last_z)
+    def _():
+        signal(met_z, (1, 1))
+
+    @pl.when(rest_t)
+    def _():
+        edges[3].start()
+        faces[0].start()
+
+    @pl.when(rest_z)
+    def _():
+        edges[5].start()
+        faces[1].start()
+
+    @pl.when(jnp.logical_or(rest_z, last_t))
+    def _():
+        edges[2].start()
+
     send_side(2)
     faces[2].start()
     opens[2].start()
@@ -524,10 +572,31 @@
     for n, pair in enumerate(PLANES):
         if n == 2:
             pl.semaphore_wait(met, 1)
-            edges[1].start()
+
+            @pl.when(rest_t)
+            def _():
+                edges[1].start()
+
         for h in range(halves):
             inner(*pair, h)
         flush()
+
+    @pl.when(first_t)
+    def _():
+        pl.semaphore_wait(met_t, 1)
+        for copy in (edges[3], edges[1], faces[0]):
+            copy.start()
+
+    @pl.when(first_z)
+    def _():
+        pl.semaphore_wait(met_z, 1)
+        edges[5].start()
+        faces[1].start()
+
+    @pl.when(jnp.logical_and(first_z, more_t))
+    def _():
+        edges[2].start()
+
     faces[2].wait_recv()
     face_terms(2, ())
     corners(0, (2,))
@@ -594,6 +663,8 @@
             pltpu.SemaphoreType.DMA,
             pltpu.SemaphoreType.DMA((7,)),
             pltpu.SemaphoreType.REGULAR,
+            pltpu.SemaphoreType.REGULAR,
+            pltpu.SemaphoreType.REGULAR,
         ],
         compiler_params=pltpu.CompilerParams(collective_id=0, has_side_effects=True),
         name="force_terms",

time: 15.9 us -> 15.5 us (0.975)
  the two profiles are of different devices: /device:TPU:1 before, /device:TPU:6 now
where the time goes in v9:
time: 15.5 us; the launch traced here: 15.3 us
  Pallas kernels  15.3 us (99%)
    pallas_call x1, Pallas kernels, per_device(): pl.pallas_call(functools.partial(force_terms, counts, depth, halves), out...  14.5 us
    pallas_call x1, Pallas kernels, per_device(): pl.pallas_call(functools.partial(expand, halves), out_shape=jax.ShapeDtyp...  0.81 us

profile of v9, /device:TPU:6, one launch (start us, length us, event | category | flops | bytes accessed | tf_op | source)
XLA Modules:
  0.0 15.3 jit_solution(17716786760335164998)
XLA Ops:
  0.0 14.5 %force_terms.1.acc = f32[512,128]{1,0:T(8,128)S(1)} custom-call(f32[4,2,3,3,16,128]{5,4,3,2,1,0:T(8,128)} %bitcast.2), custom_call_target="tpu_custom_call" | custom-call | tf_op jit(solution)/shard_map/force_terms/pallas_call | solution.py:650
  14.5 0.8 %expand.1 = f32[4,2,3,3,16,128]{5,4,3,2,1,0:T(8,128)} custom-call(f32[512,128]{1,0:T(8,128)S(1)} %force_terms.1.acc), custom_call_target="tpu_custom_call" | custom-call | tf_op jit(solution)/shard_map/expand/pallas_call | solution.py:672

commit v10 on v9

--- a/solution.py
+++ b/solution.py
@@ -139,9 +139,17 @@
         copy.start()
     barrier = pltpu.get_barrier_semaphore()
     first_t, last_t = me[0] == 0, me[0] == counts[0] - 1
-    first_z, last_z = me[1] == 0, me[1] == counts[1] - 1
-    more_t, more_z = jnp.logical_not(last_t), jnp.logical_not(last_z)
-    rest_t, rest_z = jnp.logical_not(first_t), jnp.logical_not(first_z)
+    more_t, rest_t = jnp.logical_not(last_t), jnp.logical_not(first_t)
+    middle = counts[1] // 2
+    first_z = jnp.logical_or(me[1] == 0, jnp.logical_and(me[1] == middle, rest_t))
+    last_z = jnp.logical_or(
+        me[1] == counts[1] - 1, jnp.logical_and(me[1] == middle - 1, rest_t)
+    )
+    silent = jnp.logical_or(
+        jnp.logical_and(me[1] == counts[1] - 1, rest_t),
+        jnp.logical_and(me[1] == middle - 1, me[0] > 1),
+    )
+    more_z, rest_z = jnp.logical_not(last_z), jnp.logical_not(first_z)
     one = lambda flag: jnp.where(flag, 1, 0)
 
     def signal(semaphore, *steps):
@@ -157,7 +165,7 @@
         signal(barrier, (1, 1))
         signal(barrier, (1, 1), (2, -1))
 
-    @pl.when(jnp.logical_or(more_z, first_t))
+    @pl.when(jnp.logical_not(silent))
     def _():
         signal(barrier, (1, 1), (0, -1))
 

time: 15.5 us -> 14.5 us (0.935)
  Pallas kernels: 15.3 us -> 14.3 us
    pallas_call x1, Pallas kernels: 14.5 us -> 13.5 us  [per_device(): pl.pallas_call(functools.partial(force_terms, counts, depth, halves), out...]
where the time goes in v10:
time: 14.5 us; the launch traced here: 14.3 us
  Pallas kernels  14.3 us (99%)
    pallas_call x1, Pallas kernels, per_device(): pl.pallas_call(functools.partial(force_terms, counts, depth, halves), out...  13.5 us
    pallas_call x1, Pallas kernels, per_device(): pl.pallas_call(functools.partial(expand, halves), out_shape=jax.ShapeDtyp...  0.81 us

profile of v10, /device:TPU:6, one launch (start us, length us, event | category | flops | bytes accessed | tf_op | source)
XLA Modules:
  0.0 14.3 jit_solution(17185926593755947052)
XLA Ops:
  0.0 13.5 %force_terms.1.acc = f32[512,128]{1,0:T(8,128)S(1)} custom-call(f32[4,2,3,3,16,128]{5,4,3,2,1,0:T(8,128)} %bitcast.2), custom_call_target="tpu_custom_call" | custom-call | tf_op jit(solution)/shard_map/force_terms/pallas_call | solution.py:658
  13.5 0.8 %expand.1 = f32[4,2,3,3,16,128]{5,4,3,2,1,0:T(8,128)} custom-call(f32[512,128]{1,0:T(8,128)S(1)} %force_terms.1.acc), custom_call_target="tpu_custom_call" | custom-call | tf_op jit(solution)/shard_map/expand/pallas_call | solution.py:680

commit v11 on v10

--- a/solution.py
+++ b/solution.py
@@ -426,17 +426,22 @@
         send_face(d)
     send_face(2)
     pl.semaphore_wait(barrier, expected)
-    for copy in [edges[4], edges[0], opens[1], opens[0]]:
+    signal(met, (2, -1))
+
+    @pl.when(last_t)
+    def _():
+        signal(met_t, (0, 1))
+
+    @pl.when(last_z)
+    def _():
+        signal(met_z, (1, 1))
+
+    @pl.when(jnp.logical_or(rest_z, last_t))
+    def _():
+        edges[2].start()
+
+    for copy in (edges[4], edges[0]):
         copy.start()
-    signal(met, (2, -1))
-
-    @pl.when(last_t)
-    def _():
-        signal(met_t, (0, 1))
-
-    @pl.when(last_z)
-    def _():
-        signal(met_z, (1, 1))
 
     @pl.when(rest_t)
     def _():
@@ -448,10 +453,8 @@
         edges[5].start()
         faces[1].start()
 
-    @pl.when(jnp.logical_or(rest_z, last_t))
-    def _():
-        edges[2].start()
-
+    for copy in (opens[1], opens[0]):
+        copy.start()
     send_side(2)
     faces[2].start()
     opens[2].start()

time: 14.5 us -> 13.6 us (0.938)
  the two profiles are of different devices: /device:TPU:6 before, /device:TPU:230 now
where the time goes in v11:
time: 13.6 us; the launch traced here: 13.5 us
  Pallas kernels  13.5 us (99%)
    pallas_call x1, Pallas kernels, per_device(): pl.pallas_call(functools.partial(force_terms, counts, depth, halves), out...  12.7 us
    pallas_call x1, Pallas kernels, per_device(): pl.pallas_call(functools.partial(expand, halves), out_shape=jax.ShapeDtyp...  0.81 us

profile of v11, /device:TPU:230, one launch (start us, length us, event | category | flops | bytes accessed | tf_op | source)
XLA Modules:
  0.0 13.5 jit_solution(3725060605944924128)
XLA Ops:
  0.0 12.7 %force_terms.1.acc = f32[512,128]{1,0:T(8,128)S(1)} custom-call(f32[4,2,3,3,16,128]{5,4,3,2,1,0:T(8,128)} %bitcast.2), custom_call_target="tpu_custom_call" | custom-call | tf_op jit(solution)/shard_map/force_terms/pallas_call | solution.py:661
  12.7 0.8 %expand.1 = f32[4,2,3,3,16,128]{5,4,3,2,1,0:T(8,128)} custom-call(f32[512,128]{1,0:T(8,128)S(1)} %force_terms.1.acc), custom_call_target="tpu_custom_call" | custom-call | tf_op jit(solution)/shard_map/expand/pallas_call | solution.py:683

commit v12 on v11

--- a/solution.py
+++ b/solution.py
@@ -141,14 +141,11 @@
     first_t, last_t = me[0] == 0, me[0] == counts[0] - 1
     more_t, rest_t = jnp.logical_not(last_t), jnp.logical_not(first_t)
     middle = counts[1] // 2
-    first_z = jnp.logical_or(me[1] == 0, jnp.logical_and(me[1] == middle, rest_t))
+    first_z = jnp.logical_or(me[1] == 0, jnp.logical_and(me[1] == middle, last_t))
     last_z = jnp.logical_or(
-        me[1] == counts[1] - 1, jnp.logical_and(me[1] == middle - 1, rest_t)
+        me[1] == counts[1] - 1, jnp.logical_and(me[1] == middle - 1, last_t)
     )
-    silent = jnp.logical_or(
-        jnp.logical_and(me[1] == counts[1] - 1, rest_t),
-        jnp.logical_and(me[1] == middle - 1, me[0] > 1),
-    )
+    silent = jnp.logical_and(me[1] == counts[1] - 1, rest_t)
     more_z, rest_z = jnp.logical_not(last_z), jnp.logical_not(first_z)
     one = lambda flag: jnp.where(flag, 1, 0)
 
@@ -614,15 +611,29 @@
     faces[0].wait_recv()
     face_terms(0, (2,))
     corners(1, (0, 2))
-    faces[1].wait_recv()
-    face_terms(1, (0, 2))
-    all_edges.wait_recv()
-    for d in (2, 0, 1):
-        prepare(d)
-    for d in (2, 0, 1):
-        opens[d].wait_recv()
-    for d in (2, 0, 1):
-        close(d)
+
+    def close_all():
+        for d in (2, 0, 1):
+            opens[d].wait_recv()
+        all_edges.wait_recv()
+        for d in (2, 0, 1):
+            prepare(d)
+            close(d)
+
+    def face_z():
+        faces[1].wait_recv()
+        face_terms(1, (0, 2))
+
+    @pl.when(last_z)
+    def _():
+        close_all()
+        face_z()
+
+    @pl.when(more_z)
+    def _():
+        face_z()
+        close_all()
+
     everything.wait_send()
 
 

time: 13.6 us -> 13.7 us (level)
  the two profiles are of different devices: /device:TPU:230 before, /device:TPU:6 now
where the time goes in v12:
time: 13.7 us; the launch traced here: 13.5 us
  Pallas kernels  13.5 us (99%)
    pallas_call x1, Pallas kernels, per_device(): pl.pallas_call(functools.partial(force_terms, counts, depth, halves), out...  12.7 us
    pallas_call x1, Pallas kernels, per_device(): pl.pallas_call(functools.partial(expand, halves), out_shape=jax.ShapeDtyp...  0.81 us

profile of v12, /device:TPU:6, one launch (start us, length us, event | category | flops | bytes accessed | tf_op | source)
XLA Modules:
  0.0 13.5 jit_solution(15324252671117817534)
XLA Ops:
  0.0 12.7 %force_terms.1.acc = f32[512,128]{1,0:T(8,128)S(1)} custom-call(f32[4,2,3,3,16,128]{5,4,3,2,1,0:T(8,128)} %bitcast.2), custom_call_target="tpu_custom_call" | custom-call | tf_op jit(solution)/shard_map/force_terms/pallas_call | solution.py:672
  12.7 0.8 %expand.1 = f32[4,2,3,3,16,128]{5,4,3,2,1,0:T(8,128)} custom-call(f32[512,128]{1,0:T(8,128)S(1)} %force_terms.1.acc), custom_call_target="tpu_custom_call" | custom-call | tf_op jit(solution)/shard_map/expand/pallas_call | solution.py:694

commit v13 on v12

--- a/solution.py
+++ b/solution.py
@@ -114,7 +114,7 @@
 
 
 def force_terms(
-    counts, depth, halves, hbm, acc, u, out_s, in_s, face_s, b_s, pre_s, load_sem, send, recv, met, met_t, met_z,
+    counts, depth, halves, hbm, acc, u, out_s, in_s, face_s, b_s, pre_s, send, recv, met, met_t, met_z,
 ):
     g = Lattice(depth)
     me = [lax.axis_index(a) for a in AXES]
@@ -129,14 +129,6 @@
         by = dict(zip(AXES, where))
         return (by["gx"], by["gz"], by["ta"])
 
-    loads = [
-        pltpu.make_async_copy(hbm.at[m, part, i], u.at[m, part, i], load_sem)
-        for m in range(4)
-        for part in range(2)
-        for i in range(3)
-    ]
-    for copy in loads:
-        copy.start()
     barrier = pltpu.get_barrier_semaphore()
     first_t, last_t = me[0] == 0, me[0] == counts[0] - 1
     more_t, rest_t = jnp.logical_not(last_t), jnp.logical_not(first_t)
@@ -173,6 +165,15 @@
 
     expected = 11 - 2 * one(first_t) - 2 * one(first_z) - one(jnp.logical_and(first_z, more_t))
 
+    loads = [
+        pltpu.make_async_copy(hbm.at[m, part, i], u.at[m, part, i], send)
+        for m in range(4)
+        for part in range(2)
+        for i in range(3)
+    ]
+    for copy in loads:
+        copy.start()
+
     def remote(start, rows, slot, where):
         span = slice(start, start + rows)
         return pltpu.make_async_remote_copy(
@@ -181,12 +182,12 @@
         )
 
     faces = [remote(offset("x", d), ROWS[d], d, device((d, -1))) for d in range(3)]
-    opens = [remote(offset("g", d), ROWS[d], 3 + d, device((d, 1))) for d in range(3)]
+    opens = [remote(offset("g", d), ROWS[d], 3, device((d, 1))) for d in range(3)]
     edges = [
-        remote(offset("e", k), EDGES[k], 6, device((d, 1), (n, -1)))
+        remote(offset("e", k), EDGES[k], 3, device((d, 1), (n, -1)))
         for k, (d, n) in enumerate(DIAGONALS)
     ]
-    all_edges = remote(offset("e", 0), sum(EDGES), 6, device((1, 1)))
+    arrivals = remote(offset("g", 0), TOTAL - offset("g", 0), 3, device((1, 1)))
     everything = remote(0, TOTAL, 0, device((1, 1)))
 
     def load(m, part, i, j, h):
@@ -414,7 +415,7 @@
             return g.rows(v, step + SUB - depth)
         return g.rows(v, step + (1 - depth + h if d == 1 else depth - 1 - h))
 
-    everything_in = pltpu.make_async_copy(hbm, u, load_sem)
+    everything_in = pltpu.make_async_copy(hbm, u, send)
     everything_in.wait()
     for d, n in DIAGONALS:
         pack_edges(d, n)
@@ -437,7 +438,7 @@
     def _():
         edges[2].start()
 
-    for copy in (edges[4], edges[0]):
+    for copy in (edges[4], edges[0], opens[0], opens[1]):
         copy.start()
 
     @pl.when(rest_t)
@@ -450,8 +451,6 @@
         edges[5].start()
         faces[1].start()
 
-    for copy in (opens[1], opens[0]):
-        copy.start()
     send_side(2)
     faces[2].start()
     opens[2].start()
@@ -613,9 +612,7 @@
     corners(1, (0, 2))
 
     def close_all():
-        for d in (2, 0, 1):
-            opens[d].wait_recv()
-        all_edges.wait_recv()
+        arrivals.wait_recv()
         for d in (2, 0, 1):
             prepare(d)
             close(d)
@@ -682,8 +679,7 @@
             vmem(5, 2, 3, 3, SUB),
             vmem(5, 2, 3, 3, SUB),
             pltpu.SemaphoreType.DMA,
-            pltpu.SemaphoreType.DMA,
-            pltpu.SemaphoreType.DMA((7,)),
+            pltpu.SemaphoreType.DMA((4,)),
             pltpu.SemaphoreType.REGULAR,
             pltpu.SemaphoreType.REGULAR,
             pltpu.SemaphoreType.REGULAR,

time: 13.7 us -> 13.6 us (level)
  no operation moved by 1% of the time
where the time goes in v13:
time: 13.6 us; the launch traced here: 13.5 us
  Pallas kernels  13.4 us (99%)
    pallas_call x1, Pallas kernels, per_device(): pl.pallas_call(functools.partial(force_terms, counts, depth, halves), out...  12.6 us
    pallas_call x1, Pallas kernels, per_device(): pl.pallas_call(functools.partial(expand, halves), out_shape=jax.ShapeDtyp...  0.81 us

profile of v13, /device:TPU:6, one launch (start us, length us, event | category | flops | bytes accessed | tf_op | source)
XLA Modules:
  0.0 13.5 jit_solution(17415500159414147294)
XLA Ops:
  0.0 12.6 %force_terms.1.acc = f32[512,128]{1,0:T(8,128)S(1)} custom-call(f32[4,2,3,3,16,128]{5,4,3,2,1,0:T(8,128)} %bitcast.2), custom_call_target="tpu_custom_call" | custom-call | tf_op jit(solution)/shard_map/force_terms/pallas_call | solution.py:669
  12.6 0.8 %expand.1 = f32[4,2,3,3,16,128]{5,4,3,2,1,0:T(8,128)} custom-call(f32[512,128]{1,0:T(8,128)S(1)} %force_terms.1.acc), custom_call_target="tpu_custom_call" | custom-call | tf_op jit(solution)/shard_map/expand/pallas_call | solution.py:690

commit v14 on v13

--- a/solution.py
+++ b/solution.py
@@ -139,6 +139,9 @@
     )
     silent = jnp.logical_and(me[1] == counts[1] - 1, rest_t)
     more_z, rest_z = jnp.logical_not(last_z), jnp.logical_not(first_z)
+    early = jnp.logical_and(me[1] == middle - 1, last_t)
+    late = jnp.logical_and(me[1] == middle, me[0] == counts[0] - 2)
+    vouch = jnp.logical_and(me[1] == middle - 1, me[0] == counts[0] - 2)
     one = lambda flag: jnp.where(flag, 1, 0)
 
     def signal(semaphore, *steps):
@@ -161,9 +164,13 @@
     @pl.when(more_t)
     def _():
         signal(barrier, (0, 1))
+
+    @pl.when(jnp.logical_not(jnp.logical_or(last_t, late)))
+    def _():
         signal(barrier, (0, 1), (1, -1))
 
     expected = 11 - 2 * one(first_t) - 2 * one(first_z) - one(jnp.logical_and(first_z, more_t))
+    expected = expected - one(early)
 
     loads = [
         pltpu.make_async_copy(hbm.at[m, part, i], u.at[m, part, i], send)
@@ -426,7 +433,7 @@
     pl.semaphore_wait(barrier, expected)
     signal(met, (2, -1))
 
-    @pl.when(last_t)
+    @pl.when(jnp.logical_or(last_t, vouch))
     def _():
         signal(met_t, (0, 1))
 
@@ -438,17 +445,26 @@
     def _():
         edges[2].start()
 
-    for copy in (edges[4], edges[0], opens[0], opens[1]):
+    for copy in (edges[4], edges[0]):
         copy.start()
 
+    @pl.when(jnp.logical_not(jnp.logical_or(first_t, early)))
+    def _():
+        edges[3].start()
+
+    @pl.when(rest_z)
+    def _():
+        edges[5].start()
+
+    for copy in (opens[0], opens[1]):
+        copy.start()
+
     @pl.when(rest_t)
     def _():
-        edges[3].start()
         faces[0].start()
 
     @pl.when(rest_z)
     def _():
-        edges[5].start()
         faces[1].start()
 
     send_side(2)
@@ -593,6 +609,11 @@
         pl.semaphore_wait(met_t, 1)
         for copy in (edges[3], edges[1], faces[0]):
             copy.start()
+
+    @pl.when(early)
+    def _():
+        pl.semaphore_wait(met_t, 1)
+        edges[3].start()
 
     @pl.when(first_z)
     def _():

time: 13.6 us -> 13.6 us (level)
  no operation moved by 1% of the time
where the time goes in v14:
time: 13.6 us; the launch traced here: 13.5 us
  Pallas kernels  13.5 us (99%)
    pallas_call x1, Pallas kernels, per_device(): pl.pallas_call(functools.partial(force_terms, counts, depth, halves), out...  12.6 us
    pallas_call x1, Pallas kernels, per_device(): pl.pallas_call(functools.partial(expand, halves), out_shape=jax.ShapeDtyp...  0.81 us

profile of v14, /device:TPU:6, one launch (start us, length us, event | category | flops | bytes accessed | tf_op | source)
XLA Modules:
  0.0 13.5 jit_solution(9100365358247474172)
XLA Ops:
  0.0 12.6 %force_terms.1.acc = f32[512,128]{1,0:T(8,128)S(1)} custom-call(f32[4,2,3,3,16,128]{5,4,3,2,1,0:T(8,128)} %bitcast.2), custom_call_target="tpu_custom_call" | custom-call | tf_op jit(solution)/shard_map/force_terms/pallas_call | solution.py:690
  12.7 0.8 %expand.1 = f32[4,2,3,3,16,128]{5,4,3,2,1,0:T(8,128)} custom-call(f32[512,128]{1,0:T(8,128)S(1)} %force_terms.1.acc), custom_call_target="tpu_custom_call" | custom-call | tf_op jit(solution)/shard_map/expand/pallas_call | solution.py:711

commit v15 on v14

--- a/solution.py
+++ b/solution.py
@@ -104,13 +104,21 @@
 EDGES = (8, 8, 16, 16, 8, 8)
 
 
+def group_rows(d):
+    return ROWS[d] + sum(rows for pair, rows in zip(DIAGONALS, EDGES) if pair[0] == d)
+
+
 def offset(kind, d):
-    if kind == "e":
-        return 2 * sum(ROWS) + sum(EDGES[:d])
-    return (sum(ROWS) if kind == "g" else 0) + sum(ROWS[:d])
-
-
-TOTAL = offset("e", len(DIAGONALS))
+    if kind == "x":
+        return sum(ROWS[:d])
+    if kind == "g":
+        return sum(ROWS) + sum(group_rows(k) for k in range(d))
+    own = DIAGONALS[d][0]
+    before = sum(EDGES[k] for k in range(d) if DIAGONALS[k][0] == own)
+    return offset("g", own) + ROWS[own] + before
+
+
+TOTAL = sum(ROWS) + sum(group_rows(d) for d in range(3))
 
 
 def force_terms(
@@ -189,12 +197,12 @@
         )
 
     faces = [remote(offset("x", d), ROWS[d], d, device((d, -1))) for d in range(3)]
-    opens = [remote(offset("g", d), ROWS[d], 3, device((d, 1))) for d in range(3)]
+    opens = [remote(offset("g", d), ROWS[d], 3 + d, device((d, 1))) for d in range(3)]
     edges = [
-        remote(offset("e", k), EDGES[k], 3, device((d, 1), (n, -1)))
+        remote(offset("e", k), EDGES[k], 3 + d, device((d, 1), (n, -1)))
         for k, (d, n) in enumerate(DIAGONALS)
     ]
-    arrivals = remote(offset("g", 0), TOTAL - offset("g", 0), 3, device((1, 1)))
+    arrivals = [remote(offset("g", d), group_rows(d), 3 + d, device((1, 1))) for d in range(3)]
     everything = remote(0, TOTAL, 0, device((1, 1)))
 
     def load(m, part, i, j, h):
@@ -633,8 +641,8 @@
     corners(1, (0, 2))
 
     def close_all():
-        arrivals.wait_recv()
-        for d in (2, 0, 1):
+        for d in (2, 1, 0):
+            arrivals[d].wait_recv()
             prepare(d)
             close(d)
 
@@ -700,7 +708,7 @@
             vmem(5, 2, 3, 3, SUB),
             vmem(5, 2, 3, 3, SUB),
             pltpu.SemaphoreType.DMA,
-            pltpu.SemaphoreType.DMA((4,)),
+            pltpu.SemaphoreType.DMA((6,)),
             pltpu.SemaphoreType.REGULAR,
             pltpu.SemaphoreType.REGULAR,
             pltpu.SemaphoreType.REGULAR,

time: 13.6 us -> 13.4 us (0.985)
  the two profiles are of different devices: /device:TPU:6 before, /device:TPU:113 now
where the time goes in v15:
time: 13.4 us; the launch traced here: 13.3 us
  Pallas kernels  13.3 us (99%)
    pallas_call x1, Pallas kernels, per_device(): pl.pallas_call(functools.partial(force_terms, counts, depth, halves), out...  12.5 us
    pallas_call x1, Pallas kernels, per_device(): pl.pallas_call(functools.partial(expand, halves), out_shape=jax.ShapeDtyp...  0.81 us

profile of v15, /device:TPU:113, one launch (start us, length us, event | category | flops | bytes accessed | tf_op | source)
XLA Modules:
  0.0 13.3 jit_solution(16611510874305159798)
XLA Ops:
  0.0 12.5 %force_terms.1.acc = f32[512,128]{1,0:T(8,128)S(1)} custom-call(f32[4,2,3,3,16,128]{5,4,3,2,1,0:T(8,128)} %bitcast.2), custom_call_target="tpu_custom_call" | custom-call | tf_op jit(solution)/shard_map/force_terms/pallas_call | solution.py:698
  12.5 0.8 %expand.1 = f32[4,2,3,3,16,128]{5,4,3,2,1,0:T(8,128)} custom-call(f32[512,128]{1,0:T(8,128)S(1)} %force_terms.1.acc), custom_call_target="tpu_custom_call" | custom-call | tf_op jit(solution)/shard_map/expand/pallas_call | solution.py:719

commit v16 on v15

--- a/solution.py
+++ b/solution.py
@@ -475,8 +475,8 @@
     def _():
         faces[1].start()
 
+    faces[2].start()
     send_side(2)
-    faces[2].start()
     opens[2].start()
 
     seen, pending = set(), {}

time: 13.4 us -> 13.5 us (level)
  no operation moved by 1% of the time
where the time goes in v16:
time: 13.5 us; the launch traced here: 13.3 us
  Pallas kernels  13.3 us (99%)
    pallas_call x1, Pallas kernels, per_device(): pl.pallas_call(functools.partial(force_terms, counts, depth, halves), out...  12.5 us
    pallas_call x1, Pallas kernels, per_device(): pl.pallas_call(functools.partial(expand, halves), out_shape=jax.ShapeDtyp...  0.81 us

profile of v16, /device:TPU:113, one launch (start us, length us, event | category | flops | bytes accessed | tf_op | source)
XLA Modules:
  0.0 13.3 jit_solution(6281163872331333526)
XLA Ops:
  0.0 12.5 %force_terms.1.acc = f32[512,128]{1,0:T(8,128)S(1)} custom-call(f32[4,2,3,3,16,128]{5,4,3,2,1,0:T(8,128)} %bitcast.2), custom_call_target="tpu_custom_call" | custom-call | tf_op jit(solution)/shard_map/force_terms/pallas_call | solution.py:698
  12.5 0.8 %expand.1 = f32[4,2,3,3,16,128]{5,4,3,2,1,0:T(8,128)} custom-call(f32[512,128]{1,0:T(8,128)S(1)} %force_terms.1.acc), custom_call_target="tpu_custom_call" | custom-call | tf_op jit(solution)/shard_map/expand/pallas_call | solution.py:719

commit v17 on v16

--- a/solution.py
+++ b/solution.py
@@ -453,7 +453,7 @@
     def _():
         edges[2].start()
 
-    for copy in (edges[4], edges[0]):
+    for copy in (edges[4], edges[0], faces[2]):
         copy.start()
 
     @pl.when(jnp.logical_not(jnp.logical_or(first_t, early)))
@@ -475,7 +475,6 @@
     def _():
         faces[1].start()
 
-    faces[2].start()
     send_side(2)
     opens[2].start()
 

time: 13.5 us -> 13.5 us (level)
  no operation moved by 1% of the time
where the time goes in v17:
time: 13.5 us; the launch traced here: 13.3 us
  Pallas kernels  13.3 us (99%)
    pallas_call x1, Pallas kernels, per_device(): pl.pallas_call(functools.partial(force_terms, counts, depth, halves), out...  12.5 us
    pallas_call x1, Pallas kernels, per_device(): pl.pallas_call(functools.partial(expand, halves), out_shape=jax.ShapeDtyp...  0.81 us

profile of v17, /device:TPU:113, one launch (start us, length us, event | category | flops | bytes accessed | tf_op | source)
XLA Modules:
  0.0 13.3 jit_solution(9250817163698842258)
XLA Ops:
  0.0 12.5 %force_terms.1.acc = f32[512,128]{1,0:T(8,128)S(1)} custom-call(f32[4,2,3,3,16,128]{5,4,3,2,1,0:T(8,128)} %bitcast.2), custom_call_target="tpu_custom_call" | custom-call | tf_op jit(solution)/shard_map/force_terms/pallas_call | solution.py:697
  12.5 0.8 %expand.1 = f32[4,2,3,3,16,128]{5,4,3,2,1,0:T(8,128)} custom-call(f32[512,128]{1,0:T(8,128)S(1)} %force_terms.1.acc), custom_call_target="tpu_custom_call" | custom-call | tf_op jit(solution)/shard_map/expand/pallas_call | solution.py:718
